TPU v7x, 32 devices: a whole 2x2x4 slice. The times are simulated.
32 devices in a mesh: seq: 4 (over z), nbr: 4 (over y, x), batch: 2 (over core).
Axes of the slice: x: 2, y: 2, z: 4, core: 2. Of those that a mesh axis runs over, the one named last changes fastest.
Arguments:
- hidden: bfloat16 [1024, 4096], P(('batch', 'seq'), 'nbr'), parts along dimension 0, may hold values from -6 to 6
- d_out: bfloat16 [1024, 4096], P(('batch', 'seq'), 'nbr'), parts along dimension 0, may hold values from -6 to 6
- nbr_emb: bfloat16 [192, 128, 896], P(('batch', 'seq', 'nbr')), parts along dimension 0, may hold values from -6 to 6
- slot_span: int32 [192], P(('batch', 'seq')), parts along dimension 0, may hold values from -1 to 1, as said below
- dec_gain: bfloat16 [4096], P('nbr'), may hold values from 0.5 to 1.5
- enc_gain: bfloat16 [896], replicated, may hold values from 0.5 to 1.5
- w_cond: bfloat16 [4096, 896], P('nbr'), may hold values from -0.75 to 0.75
- w_enc: bfloat16 [896, 896], replicated, may hold values from -0.1875 to 0.1875
- w_q: bfloat16 [4096, 2048], P('seq', 'nbr'), may hold values from -0.09375 to 0.09375
- w_k: bfloat16 [896, 2048], P('seq', 'nbr'), may hold values from -8 to 8
- w_v: bfloat16 [896, 2048], P('seq', 'nbr'), may hold values from -0.1875 to 0.1875
- w_o: bfloat16 [2048, 4096], P('nbr', 'seq'), may hold values from -0.125 to 0.125
Outputs:
- out: bfloat16 [1024, 4096], P(('batch', 'seq'), 'nbr'), parts along dimension 0
- d_hidden: bfloat16 [1024, 4096], P(('batch', 'seq'), 'nbr'), parts along dimension 0
- d_enc: bfloat16 [192, 128, 896], P(('batch', 'seq', 'nbr')), parts along dimension 0
- d_wo: float32 [4096, 4096], P(('batch', 'nbr'), 'seq'), parts along dimension 0
- d_wk: float32 [1792, 2048], P(('batch', 'seq'), 'nbr'), parts along dimension 0
- d_wv: float32 [1792, 2048], P(('batch', 'seq'), 'nbr'), parts along dimension 0
There are 2 independent parts, one for each index of `batch`. A program takes and returns all parts, laid end to end along the dimension named above; an argument that names none is the same for every part. Nothing has to cross between parts.
Inputs may be any that keep to these rules, and one draw needn't show every extreme that they name: `slot_span`: A slot on seq index s serves a span of seq index s, counted from 0 within its 2 spans; -1 marks an empty slot. Every span is served by 1 to 8 slots, and one span of each seq index by exactly 8. Within each seq index one nbr index has all 6 slots live.
All inputs are finite; a program needn't handle non-finite values.
Results may differ from a plain program's by a relative error of at most 0.018.
The roundings to bfloat16 on the way count: a program that leaves them out, or rounds other values in their place, can miss the bound.
Values may be sent and summed in bfloat16 or wider, within the bound.
A program may use at most 128 MiB of HBM per device.

v0:
```python
import functools

import jax
import jax.numpy as jnp
from jax import lax
from jax.experimental import pallas as pl
from jax.experimental.pallas import tpu as pltpu
from jax.sharding import PartitionSpec as P

HD = 128
CLEN = 64
NLEN = 128
KMAX = 8
BF = jnp.bfloat16
F32 = jnp.float32
MESH = pl.DeviceIdType.MESH
ANY = pl.BlockSpec(memory_space=pl.ANY)


def shifted(shard, axis, by):
    length = lax.axis_size(axis)
    pairs = [(i, i + by) for i in range(length) if 0 <= i + by < length]
    return lax.ppermute(shard, axis, pairs)


def rms_scale(values):
    return lax.rsqrt(jnp.mean(values * values, axis=-1, keepdims=True) + 1e-06)


def remote(src, dst, send, recv, dev):
    return pltpu.make_async_remote_copy(
        src_ref=src, dst_ref=dst, send_sem=send, recv_sem=recv, device_id=dev, device_id_type=MESH
    )


def cols(ref, i, width):
    return ref.at[:, pl.ds(pl.multiple_of(i * width, 128), width)]


def gather_kernel(n_seq, *refs):
    ins, outs, vm = refs[:8], refs[8:16], refs[16:24]
    lsem, osem, zs, zr, ps, pr, ns, nr = refs[24:]
    s, n, b = lax.axis_index("seq"), lax.axis_index("nbr"), lax.axis_index("batch")
    x, y, core = {"nbr": n ^ 1}, {"nbr": n ^ 2}, {"batch": 1 - b}
    right, left = {"seq": s + 1}, {"seq": s - 1}
    has_right, has_left = s + 1 < n_seq, s > 0

    def view(a, i):
        if a in (0, 1, 2):
            return cols(outs[a], i, ins[a].shape[1])
        if a == 7:
            return cols(outs[a], i, ins[a].shape[1])
        return outs[a].at[i]

    def half(a, ref, h):
        if a in (5, 6):
            w = ins[a].shape[1] // 2
            return cols(ref, h, w)
        rows = ins[a].shape[0] // 2
        return ref.at[pl.ds(h * rows, rows)]

    loads = [pltpu.make_async_copy(ins[a], vm[a], lsem.at[a]) for a in range(8)]
    for c in loads:
        c.start()
    barrier = pltpu.get_barrier_semaphore()
    for dev in (x, y, core):
        pl.semaphore_signal(barrier, inc=1, device_id=dev, device_id_type=MESH)

    for k in range(1, n_seq):
        dev = {"seq": lax.rem(s + k, n_seq)}
        pl.semaphore_signal(barrier, inc=1, device_id=dev, device_id_type=MESH)
    pl.semaphore_wait(barrier, n_seq + 2)

    def ring(a, k, d, src):
        own = s - k + 1 if d == 0 else s + k - 1
        dst = half(a, view(a, own), b)
        return remote(dst if src is None else src, dst, zs.at[a - 4, k, d], zr.at[a - 4, k, d],
                      right if d == 0 else left)

    def guard(d, k):
        if d == 0:
            return has_right & (s - (k - 1) >= 0)
        return has_left & (s + (k - 1) < n_seq)

    stores = []
    for a in (4, 7, 0, 1, 2, 3, 5, 6):
        loads[a].wait()
        c = pltpu.make_async_copy(vm[a], view(a, n if a < 4 else s), osem.at[a])
        c.start()
        stores.append(c)
        if a < 4:
            remote(vm[a], view(a, n), ns.at[a, 0], nr.at[a, 0], x).start()
            remote(vm[a], view(a, n), ns.at[a, 1], nr.at[a, 1], y).start()
        else:
            for d in (0, 1):
                @pl.when(guard(d, 1))
                def _(a=a, d=d):
                    ring(a, 1, d, half(a, vm[a], b)).start()

    def diagonal(a):
        for d, (src, dev, h) in enumerate(((n ^ 1, y, 0), (n ^ 2, x, 1))):
            full = view(a, src)
            remote(full, full, ns.at[a, d], nr.at[a, d], dev).wait_recv()
            part = half(a, full, h)
            remote(part, part, ns.at[a, 2 + d], nr.at[a, 2 + d], dev).start()

    def share(a, k, d, h):
        j = s - k if d == 0 else s + k
        part = half(a, view(a, j), h)
        return remote(part, part, ps.at[a - 4, k, d], pr.at[a - 4, k, d], core)

    def relay(a, k, d):
        valid = (s - k >= 0) if d == 0 else (s + k < n_seq)

        @pl.when(valid)
        def _():
            j = s - k if d == 0 else s + k
            part = half(a, view(a, j), b)
            remote(part, part, zs.at[a - 4, k, d], zr.at[a - 4, k, d],
                   left if d == 0 else right).wait_recv()
            share(a, k, d, b).start()

        if k + 1 < n_seq:
            @pl.when(guard(d, k + 1))
            def _():
                ring(a, k + 1, d, None).start()

    for a in (0, 1, 2):
        diagonal(a)
    for k in range(1, n_seq):
        for a in (4, 7, 5, 6):
            for d in (0, 1):
                relay(a, k, d)
        if k == 1:
            diagonal(3)
    for k in range(1, n_seq):
        for a in (4, 7, 5, 6):
            for d in (0, 1):
                @pl.when((s - k >= 0) if d == 0 else (s + k < n_seq))
                def _(a=a, k=k, d=d):
                    share(a, k, d, 1 - b).wait_recv()
                    share(a, k, d, b).wait_send()

                @pl.when(guard(d, k))
                def _(a=a, k=k, d=d):
                    ring(a, k, d, None).wait_send()
    for a in range(4):
        full = view(a, n ^ 3)
        for d in (0, 1):
            part = half(a, full, d)
            c = remote(part, part, ns.at[a, 2 + d], nr.at[a, 2 + d], x)
            c.wait_recv()
            c.wait_send()
            whole = view(a, n)
            remote(whole, whole, ns.at[a, d], nr.at[a, d], x).wait_send()
    for c in stores:
        c.wait()


def gather_all(hidden, d_out, gain, enc, w_q, w_k, w_v, w_o):
    n_seq, n_nbr = lax.axis_size("seq"), lax.axis_size("nbr")
    args = (hidden, d_out, gain, enc, w_q, w_k, w_v, w_o)
    shapes = []
    for i, v in enumerate(args):
        if i < 3:
            shape = (v.shape[0], v.shape[1] * n_nbr)
        elif i == 3:
            shape = (n_nbr,) + v.shape
        elif i < 7:
            shape = (n_seq,) + v.shape
        else:
            shape = (v.shape[0], v.shape[1] * n_seq)
        shapes.append(jax.ShapeDtypeStruct(shape, v.dtype))
    dma = pltpu.SemaphoreType.DMA
    return pl.pallas_call(
        functools.partial(gather_kernel, n_seq),
        out_shape=shapes,
        in_specs=[ANY] * 8,
        out_specs=[ANY] * 8,
        scratch_shapes=[pltpu.VMEM(v.shape, v.dtype) for v in args]
        + [dma((8,)), dma((8,)), dma((4, n_seq, 2)), dma((4, n_seq, 2)),
           dma((4, n_seq, 2)), dma((4, n_seq, 2)), dma((4, 4)), dma((4, 4))],
        compiler_params=pltpu.CompilerParams(
            collective_id=0, has_side_effects=True, vmem_limit_bytes=24 * 2**20
        ),
        name="gather_all",
    )(*args)


def exchange_kernel(n_seq, n_nbr, *refs):
    ins, outs, transit = refs[:8], refs[8:16], refs[16]
    ns, nr, zs, zr, ts, tr, fs, fr = refs[17:]
    s, n = lax.axis_index("seq"), lax.axis_index("nbr")
    x, y = {"nbr": n ^ 1}, {"nbr": n ^ 2}
    barrier = pltpu.get_barrier_semaphore()
    for d in range(1, n_nbr):
        pl.semaphore_signal(barrier, inc=1, device_id={"nbr": n ^ d}, device_id_type=MESH)
    for k in range(1, n_seq):
        pl.semaphore_signal(barrier, inc=1, device_id={"seq": lax.rem(s + k, n_seq)}, device_id_type=MESH)
    pl.semaphore_wait(barrier, n_nbr + n_seq - 2)
    h = ins[2].shape[1] // 2
    parts = (pl.ds(0, h), pl.ds(h, h))
    hops = [
        remote(ins[2].at[n ^ 3, parts[i]], transit.at[i], ts.at[i], tr.at[i], dev)
        for i, dev in enumerate((x, y))
    ]
    for c in hops:
        c.start()
    copies = []
    for a in (2, 7, 0, 1):
        for d in (1, 2, 3):
            if a == 2 and d == 3:
                continue
            peer = n ^ d
            if a == 2:
                src = ins[a].at[peer]
            elif a == 7:
                src = ins[a]
            else:
                src = cols(ins[a], peer, ins[a].shape[1] // n_nbr)
            i = 3 if a == 7 else a
            copies.append(remote(src, outs[a].at[d - 1], ns.at[i, d], nr.at[i, d], {"nbr": peer}))
    for k in range(1, n_seq):
        peer = lax.rem(s + k, n_seq)
        for a in (3, 4, 5, 6):
            if a == 3:
                src = ins[a]
            elif a == 4:
                src = cols(ins[a], peer, ins[a].shape[1] // n_seq)
            else:
                src = ins[a].at[peer]
            copies.append(remote(src, outs[a].at[k - 1], zs.at[a - 3, k], zr.at[a - 3, k], {"seq": peer}))
    for c in copies:
        c.start()
    onward = []
    for i, dev in enumerate((y, x)):
        hops[i].wait_recv()
        c = remote(transit.at[i], outs[2].at[2, parts[i]], fs.at[i], fr.at[i], dev)
        c.start()
        onward.append(c)
    for c in copies + onward:
        c.wait()
    for c in hops:
        c.wait_send()


def exchange_all(part_out, part_dn, part_enc, attended, dout_all, part_wk, part_wv, part_stat):
    n_seq, n_nbr = lax.axis_size("seq"), lax.axis_size("nbr")
    args = (part_out, part_dn, part_enc, attended, dout_all, part_wk, part_wv, part_stat)
    tokens, full = part_out.shape
    slots = part_enc.shape[1:]
    shapes = [
        (n_nbr - 1, tokens, full // n_nbr),
        (n_nbr - 1, tokens, full // n_nbr),
        (n_nbr - 1,) + slots,
        (n_seq - 1,) + attended.shape,
        (n_seq - 1, tokens, full // n_seq),
        (n_seq - 1,) + part_wk.shape[1:],
        (n_seq - 1,) + part_wv.shape[1:],
        (n_nbr - 1,) + part_stat.shape,
        (2, slots[0] // 2) + slots[1:],
    ]
    types = [BF] * 7 + [F32, BF]
    dma = pltpu.SemaphoreType.DMA
    return pl.pallas_call(
        functools.partial(exchange_kernel, n_seq, n_nbr),
        out_shape=[jax.ShapeDtypeStruct(v, k) for v, k in zip(shapes, types)],
        in_specs=[ANY] * 8,
        out_specs=[ANY] * 9,
        scratch_shapes=[dma((4, n_nbr)), dma((4, n_nbr)), dma((4, n_seq)), dma((4, n_seq))]
        + [dma((2,))] * 4,
        compiler_params=pltpu.CompilerParams(
            collective_id=1, has_side_effects=True, vmem_limit_bytes=60 * 2**20
        ),
        name="exchange_all",
    )(*args)[:8]


GROUP = 4


def project_kernel(idx, *refs):
    wk, wv, enc_o, k_o, v_o = refs[GROUP:]
    e = jnp.concatenate([r[0] for r in refs[:GROUP]], axis=0)
    enc_o[...] = e
    k_o[...] = jnp.dot(e, wk[...], preferred_element_type=F32).astype(BF)
    v_o[...] = jnp.dot(e, wv[...], preferred_element_type=F32).astype(BF)


def project(idx, enc, wk, wv):
    count, (width, local) = idx.shape[0], wk.shape
    out = lambda w: pl.BlockSpec((GROUP * NLEN, w), lambda i, idx: (i, 0))
    weight = pl.BlockSpec((width, local), lambda i, idx: (0, 0))
    slot = lambda j: pl.BlockSpec((1, NLEN, width), lambda i, idx: (idx[i * GROUP + j], 0, 0))
    return pl.pallas_call(
        project_kernel,
        out_shape=[jax.ShapeDtypeStruct((count * NLEN, w), BF) for w in (width, local, local)],
        grid_spec=pltpu.PrefetchScalarGridSpec(
            num_scalar_prefetch=1,
            grid=(count // GROUP,),
            in_specs=[slot(j) for j in range(GROUP)] + [weight, weight],
            out_specs=[out(width), out(local), out(local)],
        ),
        name="project",
    )(idx, *([enc] * GROUP), wk, wv)


NT = (((1,), (1,)), ((), ()))
TN = (((0,), (0,)), ((), ()))


def attend_kernel(counts, q_ref, k_ref, v_ref, da_ref, at_o, dq_o, dk_o, dv_o):
    q, k, v, da = q_ref[...], k_ref[...], v_ref[...], da_ref[...]
    factor = HD ** (-0.5)
    dot = functools.partial(lax.dot_general, preferred_element_type=F32)
    scores = dot(q, k, NT) * factor
    place = lax.broadcasted_iota(jnp.int32, scores.shape, 1)
    scores = jnp.where(place < counts[pl.program_id(0)] * NLEN, scores, -1e30)
    weights = jnp.exp(scores - jnp.max(scores, axis=-1, keepdims=True))
    probs = weights / jnp.sum(weights, axis=-1, keepdims=True)
    probs_b = probs.astype(BF)
    at_o[...] = jnp.dot(probs_b, v, preferred_element_type=F32).astype(BF)
    d_probs = dot(da, v, NT)
    row_dot = jnp.sum(probs * d_probs, axis=-1, keepdims=True)
    d_scores = (probs * (d_probs - row_dot) * factor).astype(BF)
    dq_o[...] = jnp.dot(d_scores, k, preferred_element_type=F32).astype(BF)
    dk_o[...] = dot(d_scores, q, TN).astype(BF)
    dv_o[...] = dot(probs_b, da, TN).astype(BF)


def attend(counts, query, keys, values, d_attn):
    tokens, local = query.shape
    spans = tokens // CLEN
    tok = pl.BlockSpec((CLEN, HD), lambda c, h, n: (c, h))
    key = pl.BlockSpec((KMAX * NLEN, HD), lambda c, h, n: (c, h))
    like = lambda v: jax.ShapeDtypeStruct(v.shape, BF)
    return pl.pallas_call(
        attend_kernel,
        out_shape=[like(query), like(query), like(keys), like(keys)],
        grid_spec=pltpu.PrefetchScalarGridSpec(
            num_scalar_prefetch=1,
            grid=(spans, local // HD),
            in_specs=[tok, key, key, tok],
            out_specs=[tok, tok, key, key],
        ),
        name="attend",
    )(counts, query, keys, values, d_attn)


def back_kernel(inv, *refs):
    wk, wv, o = refs[2 * GROUP :]
    dot = functools.partial(lax.dot_general, preferred_element_type=F32)
    dk = jnp.concatenate([r[...] for r in refs[:GROUP]], axis=0)
    dv = jnp.concatenate([r[...] for r in refs[GROUP : 2 * GROUP]], axis=0)
    part = (dot(dk, wk[...], NT) + dot(dv, wv[...], NT)).astype(BF)
    for j in range(GROUP):
        live = inv[pl.program_id(0) * GROUP + j] >= 0
        rows = part[j * NLEN : (j + 1) * NLEN]
        o[j] = jnp.where(live, rows, jnp.zeros_like(rows))


def back(inv, dk, dv, wk, wv):
    count, (width, local) = inv.shape[0], wk.shape
    row = lambda j: pl.BlockSpec((NLEN, local), lambda i, inv: (jnp.maximum(inv[i * GROUP + j], 0), 0))
    weight = pl.BlockSpec((width, local), lambda i, inv: (0, 0))
    rows = [row(j) for j in range(GROUP)]
    return pl.pallas_call(
        back_kernel,
        out_shape=jax.ShapeDtypeStruct((count, NLEN, width), BF),
        grid_spec=pltpu.PrefetchScalarGridSpec(
            num_scalar_prefetch=1,
            grid=(count // GROUP,),
            in_specs=rows + rows + [weight, weight],
            out_specs=pl.BlockSpec((GROUP, NLEN, width), lambda i, inv: (i, 0, 0)),
        ),
        name="back",
    )(inv, *([dk] * GROUP), *([dv] * GROUP), wk, wv)


def body(hidden, d_out, nbr_emb, slot_span, dec_gain, enc_gain, w_cond, w_enc, w_q, w_k, w_v, w_o):
    s, n = lax.axis_index("seq"), lax.axis_index("nbr")
    tokens, feat = hidden.shape
    spans = tokens // CLEN
    pooled = jnp.mean(hidden.astype(F32).reshape(spans, CLEN, feat), axis=1).astype(BF)
    carried = shifted(pooled[spans - 1 :], "seq", 1)
    before = jnp.concatenate([carried, pooled[: spans - 1]], axis=0)
    condition = lax.psum(jnp.dot(before, w_cond, preferred_element_type=F32), "nbr")
    slots = nbr_emb.shape[0]
    own_span = lax.dynamic_slice_in_dim(slot_span, n * slots, slots)
    lookup = (own_span[:, None] == jnp.arange(spans, dtype=jnp.int32)[None, :]).astype(F32)
    slot_cond = jnp.dot(lookup, condition, precision=lax.Precision.HIGHEST)
    inputs = nbr_emb.astype(F32) + slot_cond[:, None, :]
    width = inputs.shape[2]
    enc_normed = (inputs * rms_scale(inputs) * enc_gain.astype(F32)).astype(BF)
    mixed = jnp.dot(enc_normed.reshape(-1, width), w_enc, preferred_element_type=F32).reshape(
        inputs.shape
    )
    encoded = (inputs + jax.nn.silu(mixed)).astype(BF)
    gain_rows = jnp.broadcast_to(dec_gain[None], (32, feat))
    hid_all, dout_all, gain_all, enc_all, wq_all, wk_all, wv_all, wo_all = gather_all(
        hidden, d_out, gain_rows, encoded, w_q, w_k, w_v, w_o
    )
    local = w_q.shape[1]
    wq_all = wq_all.reshape(-1, local)
    wk_all = wk_all.reshape(-1, local)
    wv_all = wv_all.reshape(-1, local)
    enc_all = enc_all.reshape(-1, NLEN, width)
    total = slot_span.shape[0]

    member = slot_span[None, :] == jnp.arange(spans, dtype=jnp.int32)[:, None]
    ids = jnp.arange(total, dtype=jnp.int32)
    earlier = ids[None, :] < ids[:, None]
    rank = jnp.sum((member[:, None, :] & earlier[None]).astype(jnp.int32), axis=-1)
    counts = jnp.sum(member.astype(jnp.int32), axis=-1)
    chosen = member[:, None, :] & (
        rank[:, None, :] == jnp.arange(KMAX, dtype=jnp.int32)[None, :, None]
    )
    idx = jnp.sum(jnp.where(chosen, ids[None, None, :], 0), axis=-1).reshape(-1)
    base = jnp.arange(spans, dtype=jnp.int32)[:, None] * KMAX
    inv = jnp.sum(jnp.where(member, base + rank + 1, 0), axis=0) - 1

    enc_rows, keys, values = project(idx, enc_all, wk_all, wv_all)
    hf = hid_all.astype(F32)
    rstd = rms_scale(hf)
    normed = (hf * rstd * gain_all[:1].astype(F32)).astype(BF)
    query = jnp.dot(normed, wq_all, preferred_element_type=F32).astype(BF)
    d_attn = lax.dot_general(dout_all, wo_all, NT, preferred_element_type=F32).astype(BF)
    attended, d_query, d_key, d_value = attend(counts, query, keys, values, d_attn)
    part_out = jnp.dot(attended, wo_all, preferred_element_type=F32).astype(BF)
    part_dn = lax.dot_general(d_query, wq_all, NT, preferred_element_type=F32).astype(BF)
    part_enc = back(inv, d_key, d_value, wk_all, wv_all).reshape((-1,) + nbr_emb.shape)
    rows = w_k.shape[0]
    part_wk = lax.dot_general(enc_rows, d_key, TN, preferred_element_type=F32).astype(BF)
    part_wv = lax.dot_general(enc_rows, d_value, TN, preferred_element_type=F32).astype(BF)
    part_wk = part_wk.reshape(-1, rows, local)
    part_wv = part_wv.reshape(-1, rows, local)
    part_stat = jnp.sum(
        hf * (gain_all[:1].astype(F32) * part_dn.astype(F32)), axis=-1, keepdims=True
    ) / hf.shape[1]
    part_stat = jnp.broadcast_to(part_stat, (tokens, HD))
    out_r, dn_r, enc_r, att_r, col_r, wk_r, wv_r, stat_r = exchange_all(
        part_out, part_dn, part_enc, attended, dout_all, part_wk, part_wv, part_stat
    )

    def total_of(own, received):
        acc = own.astype(F32)
        for i in range(received.shape[0]):
            acc = acc + received[i].astype(F32)
        return acc

    def own_cols(v, i, w):
        return lax.dynamic_slice_in_dim(v, i * w, w, axis=1)

    def own_row(v, i):
        return lax.dynamic_index_in_dim(v, i, 0, keepdims=False)

    own_states = hidden.astype(F32)
    out = (own_states + total_of(own_cols(part_out, n, feat), out_r)).astype(BF)
    d_enc = total_of(own_row(part_enc, n), enc_r).astype(BF)
    d_wk = total_of(own_row(part_wk, s), wk_r)
    d_wv = total_of(own_row(part_wv, s), wv_r)
    piece = w_o.shape[1]
    d_wo = lax.dot_general(
        jnp.concatenate([attended[None], att_r]).reshape(-1, local),
        jnp.concatenate([own_cols(dout_all, s, piece)[None], col_r]).reshape(-1, piece),
        TN, preferred_element_type=F32)
    scaled_grad = dec_gain.astype(F32) * total_of(own_cols(part_dn, n, feat), dn_r)
    stat = total_of(part_stat, stat_r)[:, :1]
    d_hidden = d_out.astype(F32) + rstd * scaled_grad - own_states * rstd**3 * stat
    return (out, d_hidden.astype(BF), d_enc, d_wo, d_wk, d_wv)


def solution(mesh):
    placed = (
        P(("batch", "seq"), "nbr"),
        P(("batch", "seq"), "nbr"),
        P(("batch", "seq", "nbr"), None, None),
        P(("batch", "seq")),
        P("nbr"),
        P(),
        P("nbr", None),
        P(),
        P("seq", "nbr"),
        P("seq", "nbr"),
        P("seq", "nbr"),
        P("nbr", "seq"),
    )
    return jax.shard_map(
        body,
        mesh=mesh,
        in_specs=placed,
        out_specs=(
            P(("batch", "seq"), "nbr"),
            P(("batch", "seq"), "nbr"),
            P(("batch", "seq", "nbr"), None, None),
            P(("batch", "nbr"), "seq"),
            P(("batch", "seq"), "nbr"),
            P(("batch", "seq"), "nbr"),
        ),
        check_vma=False,
    )
```

profile of v0, /device:TPU:0, one launch (start us, length us, event | category | flops | bytes accessed | tf_op | source)
XLA Modules:
  0.0 273.4 jit_solution(15189038226620154730)
XLA Ops:
  0.6 0.0 copy-start
  0.6 0.0 copy-start.18
  0.7 1.2 bitcast_reduce_fusion
  1.9 5.0 %collective-permute-start = (bf16[1,1024]{1,0:T(2,128)(2,1)S(1)}, bf16[1,1024]{1,0:T(2,128)(2,1)S(1)}, u32[]{:S(2)}, u32[]{:S(2)}) collective-permute-start(bf16[1,1024]{1,0:T(2,128)(2,1)S(1)} %get-tuple-element.59), channel_id=1, source_target_pairs={{0,8},{8,16},{16,24},{1,9},{9,17},{17,25},{2,10},{10,18},{18,26},{... | collective-permute-start | bytes 6152 | tf_op jit(solution)/shard_map/ppermute | solution.py:23
  6.8 0.7 iota_compare_fusion.4
  7.5 0.1 convert_reduce_fusion
  7.6 1.4 select_reduce_fusion.1
  9.0 0.5 broadcast_add_fusion.inv
  9.5 0.1 select_reduce_fusion
  9.7 0.7 convert_element_type.162
  10.4 0.7 dynamic_slice.23
  11.1 0.6 reshape.146.idx
  11.7 0.7 convert_element_type.184
  12.4 0.3 fusion.30
  12.7 10.1 %psum.7 = f32[2,896]{1,0:T(2,128)S(1)} all-reduce(f32[2,896]{1,0:T(2,128)S(1)} %fusion.30), channel_id=1, replica_groups=mesh['seq'=4,'nbr'=4,'batch'=2] {'nbr'}, use_global_device_ids=true, to_apply=%region_2.0 | all-reduce | flops 1792 | bytes 14336 | tf_op jit(solution)/shard_map/psum | solution.py:387
  22.8 0.2 fusion.34
  23.0 0.4 multiply_reduce_fusion
  23.5 0.0 copy-start.25
  23.5 0.0 copy-start.10
  23.5 0.0 copy-start.11
  23.5 0.0 copy-start.13
  23.5 0.0 copy-start.14
  23.5 4.4 %add_convert_fusion.1.refs_3_ = bf16[6,128,896]{2,1,0:T(8,128)(2,1)S(1)} fusion(bf16[6,128,896]{2,1,0:T(8,128)(2,1)} %param.14, bf16[896,896]{1,0:T(8,128)(2,1)} %param.19, f32[896]{0:T(1024)S(1)} %convert_element_type.162, f32[6,128]{1,0:T(8,128)S(1)} %add_rsqrt_fusion, f32[6,896]{1,0:T(8,128)S(1)} %fusion.34), kind=kOutput, calls=%fused_computation.6 | convolution fusion | flops 1242071040 | bytes 4386304 | tf_op jit(solution)/shard_map/dot_general | solution.py:395
  28.0 89.0 %gather_all.1 = (bf16[128,4096]{1,0:T(8,128)(2,1)S(1)}, bf16[128,4096]{1,0:T(8,128)(2,1)S(1)}, bf16[32,4096]{1,0:T(8,128)(2,1)S(1)}, bf16[4,6,128,896]{3,2,1,0:T...) custom-call(bf16[128,1024]{1,0:T(8,128)(2,1)S(1)} %copy-done.10, ...), custom_call_target="tpu_custom_call" | custom-call | tf_op jit(solution)/shard_map/gather_all/pallas_call | solution.py:175
  117.1 0.9 copy-done.8
  118.0 1.0 copy-done.9
  119.0 0.3 fusion
  119.3 2.9 %convolution_convert_fusion.4.da_ref = bf16[128,512]{1,0:T(8,128)(2,1)} fusion(bf16[128,4096]{1,0:T(8,128)(2,1)S(1)} %get-tuple-element.37.refs_4_, bf16[512,4096]{1,0:T(8,128)(2,1)S(1)} %get-tuple-element.38), kind=kOutput, calls=%fused_computation.23 | convolution fusion | flops 536936448 | bytes 5373952 | tf_op jit(solution)/shard_map/dot_general | solution.py:427
  122.2 0.4 copy-done.2
  122.6 0.4 copy-done.4
  123.0 1.6 convolution_convert_fusion.5.q_ref
  124.6 8.8 %project.1 = (bf16[2048,896]{1,0:T(8,128)(2,1)}, bf16[2048,512]{1,0:T(8,128)(2,1)}, bf16[2048,512]{1,0:T(8,128)(2,1)}) custom-call(s32[16]{0:T(128)} %reshape.146.idx, bf16[24,128,896]{2,1,0:T(8,128)(2,1)} %bitcast.63, bf16[24,128,896]{2,1,0:T(8,128)(2,1)} %bitcast.64, bf16[24,128,896]{2,1,0:T(8,128)(2,1)} %bitcast.65, bf16[24,128,896]{2,1,0:T(8,128)(2,1)} %bitcast.66, ...), custom_call_target="tpu_custom_call" | custom-call | tf_op jit(solution)/shard_map/project/pallas_call | solution.py:295
  133.4 11.5 %attend.1 = (bf16[128,512]{1,0:T(8,128)(2,1)}, bf16[128,512]{1,0:T(8,128)(2,1)}, bf16[2048,512]{1,0:T(8,128)(2,1)}, bf16[2048,512]{1,0:T(8,128)(2,1)}) custom-call(s32[2]{0:T(128)} %get-tuple-element.53.counts, bf16[128,512]{1,0:T(8,128)(2,1)} %convolution_convert_fusion.5.q_ref, bf16[2048,512]{1,0:T(8,128)(2,1)} %get-tuple-element.35.k_ref, ...), custom_call_target="tpu_custom_call" | custom-call | tf_op jit(solution)/shard_map/attend/pallas_call | solution.py:337
  144.9 4.1 %convolution_convert_fusion.1.refs_0_ = bf16[128,4096]{1,0:T(8,128)(2,1)} fusion(bf16[128,512]{1,0:T(8,128)(2,1)} %get-tuple-element.39.refs_3_, bf16[512,4096]{1,0:T(8,128)(2,1)} %copy-done.2), kind=kOutput, calls=%fused_computation.1 | convolution fusion | flops 537395200 | bytes 5373952 | tf_op jit(solution)/shard_map/dot_general | solution.py:429
  149.1 2.5 fusion.3
  151.6 0.5 copy-done.26
  152.1 3.0 %convolution_convert_fusion.3 = bf16[896,512]{1,0:T(8,128)(2,1)} fusion(bf16[2048,896]{1,0:T(8,128)(2,1)S(1)} %copy-done.26, bf16[2048,512]{1,0:T(8,128)(2,1)S(1)} %copy-done.16), kind=kOutput, calls=%fused_computation.18 | convolution fusion | flops 1879506944 | bytes 6684672 | tf_op jit(solution)/shard_map/dot_general | solution.py:433
  155.1 3.0 %convolution_convert_fusion.2 = bf16[896,512]{1,0:T(8,128)(2,1)} fusion(bf16[2048,896]{1,0:T(8,128)(2,1)S(1)} %copy-done.26, bf16[2048,512]{1,0:T(8,128)(2,1)S(1)} %copy-done.17), kind=kOutput, calls=%fused_computation.17 | convolution fusion | flops 1879506944 | bytes 6684672 | tf_op jit(solution)/shard_map/dot_general | solution.py:434
  158.2 12.2 %back.1 = bf16[24,128,896]{2,1,0:T(8,128)(2,1)} custom-call(s32[24]{0:T(128)} %broadcast_add_fusion.inv, bf16[2048,512]{1,0:T(8,128)(2,1)} %get-tuple-element.41.refs_0_.refs_1_.refs_2_.refs_3_, bf16[2048,512]{1,0:T(8,128)(2,1)} %get-tuple-element.41.refs_0_.refs_1_.refs_2_.refs_3_, bf16[2048,512]{1,0:T(8,128)(2,1)} %get-tuple-element.41.refs_0_.refs_1_.refs_2_.refs_3_, ...), custom_call_target="tpu_custom_call" | custom-call | tf_op jit(solution)/shard_map/back/pallas_call | solution.py:367
  170.4 0.7 broadcast_in_dim.27.refs_7_
  171.1 89.0 %exchange_all.1 = (bf16[3,128,1024]{2,1,0:T(8,128)(2,1)}, bf16[3,128,1024]{2,1,0:T(8,128)(2,1)}, bf16[3,6,128,896]{3,2,1,0:T(8,128)(2,1)}, bf16[3,128,512]{2,1,0...) custom-call(bf16[128,4096]{1,0:T(8,128)(2,1)} %convolution_convert_f, ...), custom_call_target="tpu_custom_call" | custom-call | tf_op jit(solution)/shard_map/exchange_all/pallas_call | solution.py:265
  260.1 0.9 slice_bitcast_fusion.2
  261.0 1.0 dynamic-slice_bitcast_fusion
  262.0 4.5 %fusion.8 = bf16[6,128,896]{2,1,0:T(8,128)(2,1)} fusion(bf16[3,6,128,896]{3,2,1,0:T(8,128)(2,1)} %get-tuple-element.47, bf16[4,6,128,896]{3,2,1,0:T(8,128)(2,1)} %bitcast.74, s32[]{:T(128)S(6)} %select_n.31), kind=kLoop, calls=%fused_computation.19 | loop fusion | flops 5505024 | bytes 6881284 | tf_op jit(solution)/shard_map/add | solution.py:448
  266.5 0.2 fusion.28
  266.7 2.4 add_bitcast_fusion
  269.1 2.1 convolution_bitcast_fusion
  271.2 2.3 fusion.25
  (56 shorter events, 0.2 us)
Async XLA Ops:
  0.6 11.7 %copy-start = (bf16[1024,896]{1,0:T(8,128)(2,1)S(1)}, bf16[1024,896]{1,0:T(8,128)(2,1)}, u32[]{:S(2)}) copy-start(bf16[1024,896]{1,0:T(8,128)(2,1)} %param.18) | copy-start | bytes 5505028
  0.6 22.4 %copy-start.18 = (bf16[6,128,896]{2,1,0:T(8,128)(2,1)S(1)}, bf16[6,128,896]{2,1,0:T(8,128)(2,1)}, u32[]{:S(2)}) copy-start(bf16[6,128,896]{2,1,0:T(8,128)(2,1)} %param.14) | copy-start | bytes 4128772
  1.9 10.5 %collective-permute-start = (bf16[1,1024]{1,0:T(2,128)(2,1)S(1)}, bf16[1,1024]{1,0:T(2,128)(2,1)S(1)}, u32[]{:S(2)}, u32[]{:S(2)}) collective-permute-start(bf16[1,1024]{1,0:T(2,128)(2,1)S(1)} %get-tuple-element.59), channel_id=1, source_target_pairs={{0,8},{8,16},{16,24},{1,9},{9,17},{17,25},{2,10},{10,18},{18,26},{... | collective-permute-start | bytes 6152 | tf_op jit(solution)/shard_map/ppermute | solution.py:23
  23.5 4.5 %copy-start.25 = (bf16[1024]{0:T(1024)(128)(2,1)S(1)}, bf16[1024]{0:T(1024)(128)(2,1)}, u32[]{:S(2)}) copy-start(bf16[1024]{0:T(1024)(128)(2,1)} %param.16) | copy-start | bytes 6148
  23.5 4.5 %copy-start.10 = (bf16[128,1024]{1,0:T(8,128)(2,1)S(1)}, bf16[128,1024]{1,0:T(8,128)(2,1)}, u32[]{:S(2)}) copy-start(bf16[128,1024]{1,0:T(8,128)(2,1)} %refs_0_.1) | copy-start | bytes 786436
  23.5 4.5 %copy-start.11 = (bf16[1024,512]{1,0:T(8,128)(2,1)S(1)}, bf16[1024,512]{1,0:T(8,128)(2,1)}, u32[]{:S(2)}) copy-start(bf16[1024,512]{1,0:T(8,128)(2,1)} %refs_4_.1) | copy-start | bytes 3145732
  23.5 4.5 %copy-start.12 = (bf16[512,1024]{1,0:T(8,128)(2,1)S(1)}, bf16[512,1024]{1,0:T(8,128)(2,1)}, u32[]{:S(2)}) copy-start(bf16[512,1024]{1,0:T(8,128)(2,1)} %refs_7_.1) | copy-start | bytes 3145732
  23.5 4.5 %copy-start.13 = (bf16[128,1024]{1,0:T(8,128)(2,1)S(1)}, bf16[128,1024]{1,0:T(8,128)(2,1)}, u32[]{:S(2)}) copy-start(bf16[128,1024]{1,0:T(8,128)(2,1)} %refs_1_.1) | copy-start | bytes 786436
  23.5 4.5 %copy-start.14 = (bf16[224,512]{1,0:T(8,128)(2,1)S(1)}, bf16[224,512]{1,0:T(8,128)(2,1)}, u32[]{:S(2)}) copy-start(bf16[224,512]{1,0:T(8,128)(2,1)} %refs_5_.1) | copy-start | bytes 688132
  23.5 4.5 %copy-start.15 = (bf16[224,512]{1,0:T(8,128)(2,1)S(1)}, bf16[224,512]{1,0:T(8,128)(2,1)}, u32[]{:S(2)}) copy-start(bf16[224,512]{1,0:T(8,128)(2,1)} %refs_6_.1) | copy-start | bytes 688132
  117.0 0.9 copy-start.8
  118.0 1.0 copy-start.9
  118.9 3.2 %copy-start.1 = (bf16[4,6,128,896]{3,2,1,0:T(8,128)(2,1)}, bf16[4,6,128,896]{3,2,1,0:T(8,128)(2,1)S(1)}, u32[]{:S(2)}) copy-start(bf16[4,6,128,896]{3,2,1,0:T(8,128)(2,1)S(1)} %get-tuple-element.32) | copy-start | bytes 16515076
  118.9 3.7 %copy-start.2 = (bf16[512,4096]{1,0:T(8,128)(2,1)}, bf16[512,4096]{1,0:T(8,128)(2,1)S(1)}, u32[]{:S(2)}) copy-start(bf16[512,4096]{1,0:T(8,128)(2,1)S(1)} %get-tuple-element.38) | copy-start | bytes 12582916
  119.0 4.1 %copy-start.4 = (bf16[128,4096]{1,0:T(8,128)(2,1)}, bf16[128,4096]{1,0:T(8,128)(2,1)S(1)}, u32[]{:S(2)}) copy-start(bf16[128,4096]{1,0:T(8,128)(2,1)S(1)} %get-tuple-element.29) | copy-start | bytes 3145732
  119.0 5.7 %copy-start.6 = (bf16[4,1024,512]{2,1,0:T(8,128)(2,1)}, bf16[4,1024,512]{2,1,0:T(8,128)(2,1)S(1)}, u32[]{:S(2)}) copy-start(bf16[4,1024,512]{2,1,0:T(8,128)(2,1)S(1)} %get-tuple-element.31) | copy-start | bytes 12582916
  119.0 14.4 %copy-start.3 = (bf16[128,4096]{1,0:T(8,128)(2,1)}, bf16[128,4096]{1,0:T(8,128)(2,1)S(1)}, u32[]{:S(2)}) copy-start(bf16[128,4096]{1,0:T(8,128)(2,1)S(1)} %get-tuple-element.37.refs_4_) | copy-start | bytes 3145732
  144.9 4.1 %copy-start.5 = (bf16[128,4096]{1,0:T(8,128)(2,1)S(1)}, bf16[128,4096]{1,0:T(8,128)(2,1)}, u32[]{:S(2)}) copy-start(bf16[128,4096]{1,0:T(8,128)(2,1)} %copy-done.4) | copy-start | bytes 3145732
  144.9 4.1 %copy-start.7 = (bf16[4,1024,512]{2,1,0:T(8,128)(2,1)S(1)}, bf16[4,1024,512]{2,1,0:T(8,128)(2,1)}, u32[]{:S(2)}) copy-start(bf16[4,1024,512]{2,1,0:T(8,128)(2,1)} %copy-done.6) | copy-start | bytes 12582916
  144.9 4.1 %copy-start.24 = (bf16[128,512]{1,0:T(8,128)(2,1)S(1)}, bf16[128,512]{1,0:T(8,128)(2,1)}, u32[]{:S(2)}) copy-start(bf16[128,512]{1,0:T(8,128)(2,1)} %get-tuple-element.40) | copy-start | bytes 393220
  149.0 2.5 copy-start.16
  149.1 3.0 %copy-start.26 = (bf16[2048,896]{1,0:T(8,128)(2,1)S(1)}, bf16[2048,896]{1,0:T(8,128)(2,1)}, u32[]{:S(2)}) copy-start(bf16[2048,896]{1,0:T(8,128)(2,1)} %get-tuple-element.43) | copy-start | bytes 11010052
  152.1 3.0 %copy-start.17 = (bf16[2048,512]{1,0:T(8,128)(2,1)S(1)}, bf16[2048,512]{1,0:T(8,128)(2,1)}, u32[]{:S(2)}) copy-start(bf16[2048,512]{1,0:T(8,128)(2,1)} %get-tuple-element.42.refs_4_.refs_5_.refs_6_.refs_7_) | copy-start | bytes 6291460
  262.0 4.7 %copy-start.21 = (bf16[3,224,512]{2,1,0:T(8,128)(2,1)S(1)}, bf16[3,224,512]{2,1,0:T(8,128)(2,1)}, u32[]{:S(2)}) copy-start(bf16[3,224,512]{2,1,0:T(8,128)(2,1)} %get-tuple-element.50) | copy-start | bytes 2064388
  262.0 4.7 %copy-start.22 = (bf16[3,224,512]{2,1,0:T(8,128)(2,1)S(1)}, bf16[3,224,512]{2,1,0:T(8,128)(2,1)}, u32[]{:S(2)}) copy-start(bf16[3,224,512]{2,1,0:T(8,128)(2,1)} %get-tuple-element.51) | copy-start | bytes 2064388
  266.5 2.6 copy-start.23
  266.5 2.6 copy-start.27
  266.5 2.6 copy-start.28
  269.1 2.1 copy-start.19
  269.1 2.1 copy-start.20
where the time goes:
time: 274 us; the launch traced here: 273 us
  Pallas kernels  211 us (77%)
  matrix products  24.1 us (9%)
  other arithmetic  15.4 us (6%)
  blocking collectives  10.1 us (4%)
  local copies, waits for them, and re-layouts  7.33 us (3%)
  starting transfers between devices  4.96 us (2%)
    pallas_call x1, Pallas kernels, exchange_all(): pl.pallas_call(functools.partial(exchange_kernel, n_seq, n_nbr), out_shap...  89 us
    pallas_call x1, Pallas kernels, gather_all(): pl.pallas_call(functools.partial(gather_kernel, n_seq), out_shape=shapes,...  89 us
    pallas_call x1, Pallas kernels, back(): pl.pallas_call(back_kernel, out_shape=jax.ShapeDtypeStruct((count, NLEN,...  12.2 us
    pallas_call x1, Pallas kernels, attend(): pl.pallas_call(attend_kernel, out_shape=[like(query), like(query), like(k...  11.5 us
    psum x1, blocking collectives, body(): lax.psum(jnp.dot(before, w_cond, preferred_element_type=F32), 'nbr')  10.1 us
    pallas_call x1, Pallas kernels, project(): pl.pallas_call(project_kernel, out_shape=[jax.ShapeDtypeStruct((count * N...  8.75 us
    add x2, other arithmetic, total_of(): acc = acc + received[i].astype(F32)  6.85 us
  transfers between devices with their start and end apart: 1, of which 0 were waited for; matrix products, arithmetic and copies ran while one was open for 2% of the time, Pallas kernels for 0%

commit v1 on v0

v1 whole, which is shorter than its diff:
```python
import functools

import jax
import jax.numpy as jnp
from jax import lax
from jax.experimental import pallas as pl
from jax.experimental.pallas import tpu as pltpu
from jax.sharding import PartitionSpec as P

HD = 128
CLEN = 64
NLEN = 128
KMAX = 8
BF = jnp.bfloat16
F32 = jnp.float32
MESH = pl.DeviceIdType.MESH
ANY = pl.BlockSpec(memory_space=pl.ANY)
NT = (((1,), (1,)), ((), ()))
TN = (((0,), (0,)), ((), ()))
TILE = 256

dot = functools.partial(lax.dot_general, preferred_element_type=F32)


def mm(a, b):
    return jnp.dot(a, b, preferred_element_type=F32)


def remote(src, dst, send, recv, dev):
    return pltpu.make_async_remote_copy(
        src_ref=src, dst_ref=dst, send_sem=send, recv_sem=recv, device_id=dev, device_id_type=MESH
    )


def cols(ref, i, width):
    return ref.at[:, pl.ds(pl.multiple_of(i * width, 128), width)]


def rows_of(ref, i, count):
    return ref.at[pl.ds(pl.multiple_of(i * count, 8), count)]


def tiles(count, step, body):
    def one(t, _):
        body(pl.multiple_of(t * step, step))
        return 0

    lax.fori_loop(0, count // step, one, 0)


def layer_kernel(n_seq, n_nbr, names, *refs):
    hidden, d_out, gain, emb, span, e_gain, w_cond, w_enc, w_q, w_k, w_v, w_o = refs[:12]
    out_o, dh_o, denc_o, dwo_o, dwk_o, dwv_o = refs[12:18]
    S = dict(zip(names, refs[18:]))
    hid, dout, gains, wq, wo, wkv = (S[k] for k in ("hid", "dout", "gains", "wq", "wo", "wkv"))
    enc, enct, kv, big, norm, rst = (S[k] for k in ("enc", "enct", "kv", "big", "norm", "rst"))
    e1, e2, e3, po, pd = (S[k] for k in ("e1", "e2", "e3", "po", "pd"))
    ro, rd, q_s, da_s, dq_s = (S[k] for k in ("ro", "rd", "q", "da", "dq"))
    att, dcol, pw, wr, dwo, dwf = (S[k] for k in ("att", "dcol", "pw", "wr", "dwo", "dwf"))
    emb_v, cond_v, enc_v, pool = (S[k] for k in ("emb", "cond", "wenc", "pool"))
    cpart, crecv, st = (S[k] for k in ("cpart", "crecv", "st"))
    lsem, osem, zs, zr, ps, pr = (S[k] for k in ("lsem", "osem", "zs", "zr", "ps", "pr"))
    ns, nr, es, er, ss, sr = (S[k] for k in ("ns", "nr", "es", "er", "ss", "sr"))
    us, ur, ks, kr = (S[k] for k in ("us", "ur", "ks", "kr"))

    s, n, b = lax.axis_index("seq"), lax.axis_index("nbr"), lax.axis_index("batch")
    x, y, core, diag = {"nbr": n ^ 1}, {"nbr": n ^ 2}, {"batch": 1 - b}, {"nbr": n ^ 3}
    right, left = {"seq": s + 1}, {"seq": s - 1}
    has_right, has_left = s + 1 < n_seq, s > 0
    tokens, feat = hidden.shape
    spans = tokens // CLEN
    slots, width = emb.shape[0], emb.shape[2]
    total = slots * n_nbr
    local = w_q.shape[1]
    heads = local // HD
    half_slots = slots // 2
    unit = half_slots * NLEN
    wr_q, wr_k, piece = w_q.shape[0], w_k.shape[0], w_o.shape[1]

    own = {
        "h": cols(hid, n, feat), "d": cols(dout, n, feat), "g": gains.at[n],
        "k": rows_of(wkv, s, wr_k).at[:, pl.ds(0, local)],
        "v": rows_of(wkv, s, wr_k).at[:, pl.ds(local, local)],
        "q": rows_of(wq, s, wr_q), "o": cols(wo, s, piece),
    }
    source = {"h": hidden, "d": d_out, "g": gain, "k": w_k, "v": w_v, "q": w_q, "o": w_o}
    loads = {
        k: pltpu.make_async_copy(source[k], own[k], lsem.at[i]) for i, k in enumerate(("h", "d", "g", "k", "v", "q", "o"))
    }
    loads["c"] = pltpu.make_async_copy(w_cond, cond_v, lsem.at[7])
    loads["e"] = pltpu.make_async_copy(emb, emb_v, lsem.at[8])
    loads["w"] = pltpu.make_async_copy(w_enc, enc_v, lsem.at[9])
    for k in ("h", "k", "v", "q", "g", "c", "d", "e", "w", "o"):
        loads[k].start()

    barrier = pltpu.get_barrier_semaphore()
    for dev in (x, y, diag, core):
        pl.semaphore_signal(barrier, inc=1, device_id=dev, device_id_type=MESH)
    for k in range(1, n_seq):
        pl.semaphore_signal(barrier, inc=1, device_id={"seq": lax.rem(s + k, n_seq)}, device_id_type=MESH)

    loads["h"].wait()
    means = []
    for c in range(spans):
        part = cols(hid, n, feat)[c * CLEN : (c + 1) * CLEN, :].astype(F32)
        means.append((jnp.sum(part, axis=0, keepdims=True) / CLEN).astype(BF).astype(F32))
    pool[0] = jnp.broadcast_to(means[spans - 1], pool.shape[1:])
    pl.semaphore_wait(barrier, n_seq + 3)

    def carry(dev):
        return remote(pool.at[0], pool.at[1], ss.at[0], sr.at[0], dev)

    @pl.when(has_right)
    def _():
        carry(right).start()

    order = ("k", "v", "q", "o")

    def block(a, j):
        if a == "k":
            return rows_of(wkv, j, wr_k).at[:, pl.ds(0, local)]
        if a == "v":
            return rows_of(wkv, j, wr_k).at[:, pl.ds(local, local)]
        if a == "q":
            return rows_of(wq, j, wr_q)
        return cols(wo, j, piece)

    def half(a, j, h):
        if a in ("k", "v"):
            w = local // 2
            base = 0 if a == "k" else local
            return rows_of(wkv, j, wr_k).at[:, pl.ds(pl.multiple_of(base + h * w, 128), w)]
        if a == "q":
            c = wr_q // 2
            return wq.at[pl.ds(pl.multiple_of(j * wr_q + h * c, 8), c)]
        c = local // 2
        return wo.at[pl.ds(pl.multiple_of(h * c, 8), c), pl.ds(pl.multiple_of(j * piece, 128), piece)]

    def ring(a, k, d):
        j = s - k + 1 if d == 0 else s + k - 1
        i = order.index(a)
        part = half(a, j, b)
        return remote(part, part, zs.at[i, k, d], zr.at[i, k, d], right if d == 0 else left)

    def guard(d, k):
        if d == 0:
            return has_right & (s - (k - 1) >= 0)
        return has_left & (s + (k - 1) < n_seq)

    def valid(d, k):
        return (s - k >= 0) if d == 0 else (s + k < n_seq)

    def launch(a):
        loads[a].wait()
        for d in (0, 1):
            @pl.when(guard(d, 1))
            def _(a=a, d=d):
                ring(a, 1, d).start()

    def share(a, k, d, h):
        j = s - k if d == 0 else s + k
        i = order.index(a)
        part = half(a, j, h)
        return remote(part, part, ps.at[i, k, d], pr.at[i, k, d], core)

    def relay(a, k):
        i = order.index(a)
        for d in (0, 1):
            @pl.when(valid(d, k))
            def _(d=d):
                part = half(a, s - k if d == 0 else s + k, b)
                remote(part, part, zs.at[i, k, d], zr.at[i, k, d], left if d == 0 else right).wait_recv()
                share(a, k, d, b).start()

            if k + 1 < n_seq:
                @pl.when(guard(d, k + 1))
                def _(d=d):
                    ring(a, k + 1, d).start()

    def arrived(a):
        for k in range(1, n_seq):
            for d in (0, 1):
                @pl.when(valid(d, k))
                def _(k=k, d=d):
                    share(a, k, d, 1 - b).wait_recv()

    def wave(w, skip=()):
        for a, lag in (("k", 0), ("v", 0), ("q", 1), ("o", 2)):
            if 1 <= w - lag < n_seq and a not in skip:
                relay(a, w - lag)

    for a in ("k", "v", "q"):
        launch(a)

    def pair(key, i):
        ref = own[key]
        return [remote(ref, ref, ns.at[i, d], nr.at[i, d], dev) for d, dev in enumerate((x, y))]

    for c in pair("h", 0):
        c.start()
    loads["g"].wait()
    gain_sends = [
        remote(own["g"], own["g"], ns.at[2, d], nr.at[2, d], dev) for d, dev in enumerate((x, y, diag))
    ]
    for c in gain_sends:
        c.start()

    @pl.when(has_left)
    def _():
        carry(left).wait_recv()

    @pl.when(jnp.logical_not(has_left))
    def _():
        pool[1] = jnp.zeros(pool.shape[1:], F32)

    place = lax.broadcasted_iota(jnp.int32, pool.shape[1:], 0)
    before = pool[1]
    for c in range(1, spans):
        before = jnp.where(place == c, jnp.broadcast_to(means[c - 1], before.shape), before)
    loads["c"].wait()
    cpart[...] = mm(before.astype(BF), cond_v[...])
    sums = [remote(cpart, crecv.at[d], ss.at[1 + d], sr.at[1 + d], dev) for d, dev in enumerate((x, y, diag))]
    for c in sums:
        c.start()
    loads["d"].wait()
    for c in pair("d", 1):
        c.start()
    for c in sums:
        c.wait_recv()
    condition = cpart[...] + crecv[0] + crecv[1] + crecv[2]

    def slot_rows(m, j):
        return pl.ds(pl.multiple_of((m * slots + j) * NLEN, NLEN), NLEN)

    def slot_copy(src, j, i, dev):
        part = enc.at[slot_rows(src, j)]
        return remote(part, part, es.at[j, i], er.at[j, i], dev)

    loads["e"].wait()
    loads["w"].wait()
    gain_row = e_gain[...].astype(F32)
    for j in range(slots):
        mark = jnp.full((1, width), span[n * slots + j], jnp.int32)
        vals = emb_v[j].astype(F32)
        for c in range(spans):
            vals = vals + jnp.where(mark == c, condition[c : c + 1], 0.0)
        scale = lax.rsqrt(jnp.mean(vals * vals, axis=-1, keepdims=True) + 1e-06)
        mixed = mm((vals * scale * gain_row).astype(BF), enc_v[...])
        enc[slot_rows(n, j), :] = (vals + mixed / (1.0 + jnp.exp(-mixed))).astype(BF)
        slot_copy(n, j, 0, x).start()
        slot_copy(n, j, 1, y).start()
        if j == half_slots:
            wave(1)
            launch("o")

    def diagonal(ref, i):
        c = tokens // 2
        for d, (src, dev) in enumerate(((n ^ 1, y), (n ^ 2, x))):
            full = cols(ref, src, feat)
            remote(full, full, ns.at[i, d], nr.at[i, d], dev).wait_recv()
            part = full.at[pl.ds(d * c, c)]
            remote(part, part, ns.at[i, 2 + d], nr.at[i, 2 + d], dev).start()

    def diagonal_done(ref, i):
        c = tokens // 2
        for d in (0, 1):
            part = cols(ref, n ^ 3, feat).at[pl.ds(d * c, c)]
            remote(part, part, ns.at[i, 2 + d], nr.at[i, 2 + d], x).wait()

    def pass_on(j):
        for d, (src, dev) in enumerate(((n ^ 1, y), (n ^ 2, x))):
            slot_copy(src, j, d, dev).wait_recv()
            if j % 2 == d:
                slot_copy(src, j, 2, dev).start()

    def project(m, j):
        at = pl.multiple_of((m * slots + j) * NLEN, NLEN)
        slot = pl.ds(m * slots + j, half_slots)
        block_rows = enc[pl.ds(at, unit), :]
        enct[:, pl.ds(at, unit)] = block_rows.T

        def tile(c):
            res = mm(enc[pl.ds(at, unit), :], wkv[:, pl.ds(c, TILE)]).astype(BF)
            kv[slot, :, pl.ds(c, TILE)] = res.reshape(half_slots, NLEN, TILE)

        tiles(2 * local, TILE, tile)

    diagonal(hid, 0)
    diagonal(dout, 1)
    wave(2)
    for j in range(half_slots):
        pass_on(j)
    diagonal_done(hid, 0)
    diagonal_done(dout, 1)
    for c in gain_sends:
        c.wait_recv()

    def norm_rows(r):
        part = hid[pl.ds(r, 32), :].astype(F32)
        scale = lax.rsqrt(jnp.mean(part * part, axis=-1, keepdims=True) + 1e-06)
        rst[pl.ds(r, 32), :] = jnp.broadcast_to(scale, (32, HD))
        for m in range(n_nbr):
            vals = hid[pl.ds(r, 32), m * feat : (m + 1) * feat].astype(F32) * scale * gains[m, 0:1].astype(F32)
            norm[pl.ds(r, 32), m * feat : (m + 1) * feat] = vals.astype(BF)

    tiles(tokens, 32, norm_rows)
    wave(3)
    for w in range(4, n_seq):
        wave(w)
    for j in range(half_slots, slots):
        pass_on(j)
    arrived("k")
    arrived("v")
    for m in (n, n ^ 1, n ^ 2):
        project(m, 0)
    wave(n_seq)
    for m in (n, n ^ 1, n ^ 2):
        project(m, half_slots)
    for j in range(slots):
        slot_copy(n ^ 3, j, 2, x).wait_recv()
        if (j + 1) % half_slots == 0:
            project(n ^ 3, j + 1 - half_slots)
    arrived("q")

    def query(c):
        q_s[:, pl.ds(c, TILE)] = mm(norm[...], wq[:, pl.ds(c, TILE)]).astype(BF)

    tiles(local, TILE, query)

    ids = [span[j] for j in range(total)]
    run = [jnp.int32(0)] * spans
    inv = []
    for j in range(total):
        at = jnp.int32(-1)
        for c in range(spans):
            hit = (ids[j] == c).astype(jnp.int32)
            at = at + hit * (c * KMAX + 1 + run[c])
            run[c] = run[c] + hit
        inv.append(at)
    for i in range(spans * KMAX):
        at = jnp.int32(0)
        for j in range(1, total):
            at = at + (inv[j] == i).astype(jnp.int32) * j
        big[i] = kv[at]
    wave(n_seq + 1)
    arrived("o")

    def z_sends():
        found = []
        for k in range(1, n_seq):
            peer = lax.rem(s + k, n_seq)
            found.append(remote(cols(dout, peer, piece), rows_of(dcol, s, tokens), ks.at[0, k], kr.at[0, k], {"seq": peer}))
        return found

    dcol_sends = z_sends()
    for c in dcol_sends:
        c.start()
    dcol[pl.ds(pl.multiple_of(s * tokens, tokens), tokens), :] = dout[:, pl.ds(pl.multiple_of(s * piece, 128), piece)]

    def d_context(c):
        da_s[:, pl.ds(c, TILE)] = dot(dout[...], wo[pl.ds(c, TILE), :], NT).astype(BF)

    tiles(local, TILE, d_context)

    keys = KMAX * NLEN
    factor = HD ** (-0.5)
    tok0 = pl.multiple_of(s * tokens, tokens)

    def head(h, _):
        hc = pl.ds(pl.multiple_of(h * HD, HD), HD)
        vc = pl.ds(pl.multiple_of(local + h * HD, HD), HD)
        for c in range(spans):
            tr, kr_, gr = pl.ds(c * CLEN, CLEN), pl.ds(c * KMAX, KMAX), pl.ds((spans + c) * KMAX, KMAX)
            q, da = q_s[tr, hc], da_s[tr, hc]
            k, v = big[kr_, :, hc].reshape(keys, HD), big[kr_, :, vc].reshape(keys, HD)
            scores = dot(q, k, NT) * factor
            spot = lax.broadcasted_iota(jnp.int32, scores.shape, 1)
            scores = jnp.where(spot < run[c] * NLEN, scores, -1e30)
            weights = jnp.exp(scores - jnp.max(scores, axis=-1, keepdims=True))
            probs = weights / jnp.sum(weights, axis=-1, keepdims=True)
            probs_b = probs.astype(BF)
            att[pl.ds(pl.multiple_of(tok0 + c * CLEN, CLEN), CLEN), hc] = mm(probs_b, v).astype(BF)
            d_probs = dot(da, v, NT)
            row_dot = jnp.sum(probs * d_probs, axis=-1, keepdims=True)
            d_scores = (probs * (d_probs - row_dot) * factor).astype(BF)
            dq_s[tr, hc] = mm(d_scores, k).astype(BF)
            big[gr, :, hc] = dot(d_scores, q, TN).astype(BF).reshape(KMAX, NLEN, HD)
            big[gr, :, vc] = dot(probs_b, da, TN).astype(BF).reshape(KMAX, NLEN, HD)
        return 0

    lax.fori_loop(0, heads, head, 0)

    att_own = rows_of(att, s, tokens)
    att_sends = [
        remote(att_own, att_own, ks.at[1, k], kr.at[1, k], {"seq": lax.rem(s + k, n_seq)}) for k in range(1, n_seq)
    ]
    for c in att_sends:
        c.start()

    for j in range(total):
        vals = big[spans * KMAX + jnp.clip(inv[j], 0, spans * KMAX - 1)]
        mark = jnp.full(vals.shape, inv[j], jnp.int32)
        kv[j] = jnp.where(mark >= 0, vals.astype(F32), 0.0).astype(BF)

    class Sum:
        def __init__(self, i, route, part, first, forward, last):
            self.i, self.part, self.r = i, part, (forward, first, last)
            self.near, self.far = (n ^ 1, n ^ 2) if route == 0 else (n ^ 2, n ^ 1)

        def copy(self, step):
            m = (n ^ 3, self.near, self.far)[step]
            dev = {"nbr": self.far if step == 2 else self.near}
            return remote(self.part(m), self.r[step], us.at[self.i, step], ur.at[self.i, step], dev)

        def second(self):
            self.copy(0).wait_recv()
            mine = self.part(self.far)
            mine[...] = (mine[...].astype(F32) + self.r[0][...].astype(F32)).astype(BF)
            self.copy(2).start()

        def result(self):
            self.copy(1).wait_recv()
            self.copy(2).wait_recv()
            return self.part(n)[...].astype(F32) + self.r[1][...].astype(F32) + self.r[2][...].astype(F32)

    enc_sums = [
        Sum(j, 0 if j < half_slots else 1, lambda m, j=j: big.at[m * slots + j, :, pl.ds(0, width)], e1.at[j], e2.at[j], e3.at[j])
        for j in range(slots)
    ]
    hr = tokens // 2
    out_sums = [
        Sum(slots + h, h, lambda m, h=h: po.at[m, pl.ds(h * hr, hr)], ro.at[0, h], ro.at[1, h], ro.at[2, h])
        for h in (0, 1)
    ]
    dn_sums = [
        Sum(slots + 2 + h, h, lambda m, h=h: pd.at[m, pl.ds(h * hr, hr)], rd.at[0, h], rd.at[1, h], rd.at[2, h])
        for h in (0, 1)
    ]

    def back(m, j):
        slot = pl.ds(m * slots + j, half_slots)
        vals = kv[slot].reshape(unit, 2 * local)
        for c in range(0, width, TILE):
            w = min(TILE, width - c)
            big[slot, :, c : c + w] = dot(vals, wkv[c : c + w, :], NT).astype(BF).reshape(half_slots, NLEN, w)

    sets = (range(0, half_slots), range(half_slots, slots))
    for h in (0, 1):
        back(n ^ 3, h * half_slots)
        for j in sets[h]:
            enc_sums[j].copy(0).start()

    def d_weights(c):
        pw[:, pl.ds(c, TILE)] = mm(enct[...], kv[:, :, pl.ds(c, TILE)].reshape(total * NLEN, TILE)).astype(BF)

    tiles(2 * local, TILE, d_weights)
    w_sends = []
    for k in range(1, n_seq):
        peer = lax.rem(s + k, n_seq)
        w_sends.append(remote(rows_of(pw, peer, wr_k), wr.at[k], ks.at[2, k], kr.at[2, k], {"seq": peer}))
    for c in w_sends:
        c.start()

    for h in (0, 1):
        back((n ^ 1, n ^ 2)[h], h * half_slots)
        for j in sets[h]:
            enc_sums[j].copy(1).start()

    def out_part(m):
        def tile(c):
            wc = pl.ds(pl.multiple_of(m * feat + c, TILE), TILE)
            po[m, :, pl.ds(c, TILE)] = mm(att[pl.ds(tok0, tokens), :], wo[:, wc]).astype(BF)

        tiles(feat, TILE, tile)

    def dn_part(m):
        def tile(c):
            wc = pl.ds(pl.multiple_of(m * feat + c, TILE), TILE)
            pd[m, :, pl.ds(c, TILE)] = dot(dq_s[...], wq[wc, :], NT).astype(BF)

        tiles(feat, TILE, tile)

    for make, group in ((out_part, out_sums), (dn_part, dn_sums)):
        make(n ^ 3)
        for u in group:
            u.copy(0).start()
        make(n ^ 1)
        make(n ^ 2)
        for u in group:
            u.copy(1).start()
        make(n)

    def stat_rows(r):
        acc = jnp.zeros((32, 1), F32)
        for m in range(n_nbr):
            vals = hid[pl.ds(r, 32), m * feat : (m + 1) * feat].astype(F32)
            grad = gains[m, 0:1].astype(F32) * pd[m, pl.ds(r, 32), :].astype(F32)
            acc = acc + jnp.sum(vals * grad, axis=-1, keepdims=True)
        rows = jnp.broadcast_to(acc / (n_nbr * feat), (32, HD))
        st[0, pl.ds(r, 32), :] = rows

    tiles(tokens, 32, stat_rows)
    st[4] = st[0].T
    stat_sends = [
        remote(st.at[4, pl.ds(0, 8)], st.at[1 + d, pl.ds(0, 8)], ss.at[4 + d], sr.at[4 + d], dev)
        for d, dev in enumerate((x, y, diag))
    ]
    for c in stat_sends:
        c.start()

    for h in (0, 1):
        back((n ^ 2, n ^ 1)[h], h * half_slots)
    for i in range(half_slots):
        enc_sums[i].second()
        enc_sums[half_slots + i].second()
    for h in (0, 1):
        back(n, h * half_slots)
    for u in out_sums + dn_sums:
        u.second()

    writes = []

    def write(src, dst):
        c = pltpu.make_async_copy(src, dst, osem.at[len(writes)])
        c.start()
        writes.append(c)

    for c in dcol_sends + att_sends:
        c.wait_recv()

    step = min(TILE, piece)

    def d_out_weights(c):
        dwo[:, pl.ds(c, step)] = dot(att[...], dcol[:, pl.ds(c, step)], TN)

    tiles(piece, step, d_out_weights)
    write(dwo, dwo_o)

    for c in w_sends:
        c.wait_recv()
    acc = rows_of(pw, s, wr_k)[...].astype(F32)
    for k in range(1, n_seq):
        acc = acc + wr[k].astype(F32)
    dwf[...] = acc
    write(dwf.at[:, pl.ds(0, local)], dwk_o)
    write(dwf.at[:, pl.ds(local, local)], dwv_o)

    for i in range(half_slots):
        for j in (i, half_slots + i):
            e1[j] = enc_sums[j].result().astype(BF)
            write(e1.at[j], denc_o.at[j])
    for h, u in enumerate(out_sums):
        vals = cols(hid, n, feat)[h * hr : (h + 1) * hr, :].astype(F32)
        ro[0, h] = (vals + u.result()).astype(BF)
        write(ro.at[0, h], out_o.at[pl.ds(h * hr, hr)])
    for c in stat_sends:
        c.wait_recv()
    stat_row = st[4, 0:1] + st[1, 0:1] + st[2, 0:1] + st[3, 0:1]
    stat = jnp.broadcast_to(stat_row, (tokens, tokens)).T
    for h, u in enumerate(dn_sums):
        rr = slice(h * hr, (h + 1) * hr)
        vals = cols(hid, n, feat)[rr, :].astype(F32)
        grad = gains[n, 0:1].astype(F32) * u.result()
        scale = rst[rr, 0:1]
        res = cols(dout, n, feat)[rr, :].astype(F32) + scale * grad - vals * scale**3 * stat[rr, 0:1]
        rd[0, h] = res.astype(BF)
        write(rd.at[0, h], dh_o.at[pl.ds(h * hr, hr)])

    @pl.when(has_right)
    def _():
        carry(right).wait_send()

    for a in order:
        for k in range(1, n_seq):
            for d in (0, 1):
                @pl.when(valid(d, k))
                def _(a=a, k=k, d=d):
                    share(a, k, d, b).wait_send()

                @pl.when(guard(d, k))
                def _(a=a, k=k, d=d):
                    ring(a, k, d).wait_send()
    for c in pair("h", 0) + pair("d", 1) + gain_sends + sums + stat_sends + dcol_sends + att_sends + w_sends:
        c.wait_send()
    for j in range(slots):
        for i in range(3):
            slot_copy(n, j, i, x).wait_send()
    for u in enc_sums + out_sums + dn_sums:
        for i in range(3):
            u.copy(i).wait_send()
    for c in writes:
        c.wait()


def layer(hidden, d_out, gain, emb, span, e_gain, w_cond, w_enc, w_q, w_k, w_v, w_o):
    n_seq, n_nbr = lax.axis_size("seq"), lax.axis_size("nbr")
    args = (hidden, d_out, gain, emb, span, e_gain, w_cond, w_enc, w_q, w_k, w_v, w_o)
    tokens, feat = hidden.shape
    slots, _, width = emb.shape
    total = slots * n_nbr
    local, piece, wr_k = w_q.shape[1], w_o.shape[1], w_k.shape[0]
    spans = tokens // CLEN
    full = feat * n_nbr
    vm = pltpu.VMEM
    dma = pltpu.SemaphoreType.DMA
    scratch = dict(
        hid=vm((tokens, full), BF), dout=vm((tokens, full), BF), gains=vm((n_nbr,) + gain.shape, BF),
        wq=vm((full, local), BF), wo=vm((local, full), BF), wkv=vm((width, 2 * local), BF),
        enc=vm((total * NLEN, width), BF), enct=vm((width, total * NLEN), BF),
        kv=vm((total, NLEN, 2 * local), BF), big=vm((2 * spans * KMAX, NLEN, 2 * local), BF),
        norm=vm((tokens, full), BF), rst=vm((tokens, HD), F32),
        e1=vm(emb.shape, BF), e2=vm(emb.shape, BF), e3=vm(emb.shape, BF),
        po=vm((n_nbr, tokens, feat), BF), pd=vm((n_nbr, tokens, feat), BF),
        ro=vm((3, 2, tokens // 2, feat), BF), rd=vm((3, 2, tokens // 2, feat), BF),
        q=vm((tokens, local), BF), da=vm((tokens, local), BF), dq=vm((tokens, local), BF),
        att=vm((n_seq * tokens, local), BF), dcol=vm((n_seq * tokens, piece), BF),
        pw=vm((width, 2 * local), BF), wr=vm((n_seq, wr_k, 2 * local), BF),
        dwo=vm((local, piece), F32), dwf=vm((wr_k, 2 * local), F32),
        emb=vm(emb.shape, BF), cond=vm(w_cond.shape, BF), wenc=vm(w_enc.shape, BF),
        pool=vm((2, 8, feat), F32), cpart=vm((8, width), F32), crecv=vm((3, 8, width), F32),
        st=vm((5, tokens, HD), F32),
        lsem=dma((10,)), osem=dma((slots + 8,)),
        zs=dma((4, n_seq, 2)), zr=dma((4, n_seq, 2)), ps=dma((4, n_seq, 2)), pr=dma((4, n_seq, 2)),
        ns=dma((3, 4)), nr=dma((3, 4)), es=dma((slots, 3)), er=dma((slots, 3)),
        ss=dma((7,)), sr=dma((7,)), us=dma((slots + 4, 3)), ur=dma((slots + 4, 3)),
        ks=dma((3, n_seq)), kr=dma((3, n_seq)),
    )
    specs = [ANY] * 12
    specs[4] = pl.BlockSpec(memory_space=pltpu.SMEM)
    specs[5] = pl.BlockSpec(memory_space=pltpu.VMEM)
    shapes = [
        jax.ShapeDtypeStruct(hidden.shape, BF), jax.ShapeDtypeStruct(hidden.shape, BF),
        jax.ShapeDtypeStruct(emb.shape, BF), jax.ShapeDtypeStruct(w_o.shape, F32),
        jax.ShapeDtypeStruct(w_k.shape, F32), jax.ShapeDtypeStruct(w_v.shape, F32),
    ]
    return pl.pallas_call(
        functools.partial(layer_kernel, n_seq, n_nbr, tuple(scratch)),
        out_shape=shapes,
        in_specs=specs,
        out_specs=[ANY] * 6,
        scratch_shapes=list(scratch.values()),
        compiler_params=pltpu.CompilerParams(
            collective_id=0, has_side_effects=True, vmem_limit_bytes=67043328
        ),
        name="layer",
    )(*args)


def body(hidden, d_out, nbr_emb, slot_span, dec_gain, enc_gain, w_cond, w_enc, w_q, w_k, w_v, w_o):
    gain = jnp.broadcast_to(dec_gain[None], (16, dec_gain.shape[0]))
    return tuple(layer(
        hidden, d_out, gain, nbr_emb, slot_span, enc_gain[None], w_cond, w_enc, w_q, w_k, w_v, w_o
    ))


def solution(mesh):
    placed = (
        P(("batch", "seq"), "nbr"),
        P(("batch", "seq"), "nbr"),
        P(("batch", "seq", "nbr"), None, None),
        P(("batch", "seq")),
        P("nbr"),
        P(),
        P("nbr", None),
        P(),
        P("seq", "nbr"),
        P("seq", "nbr"),
        P("seq", "nbr"),
        P("nbr", "seq"),
    )
    return jax.shard_map(
        body,
        mesh=mesh,
        in_specs=placed,
        out_specs=(
            P(("batch", "seq"), "nbr"),
            P(("batch", "seq"), "nbr"),
            P(("batch", "seq", "nbr"), None, None),
            P(("batch", "nbr"), "seq"),
            P(("batch", "seq"), "nbr"),
            P(("batch", "seq"), "nbr"),
        ),
        check_vma=False,
    )
```

time: 274 us -> 208 us (0.76)
  matrix products: 24.1 us -> 0 us
  Pallas kernels: 211 us -> 195 us
  other arithmetic: 15.4 us -> 0 us
  blocking collectives: 10.1 us -> 0 us
  starting transfers between devices: 4.96 us -> 0 us
  local copies, waits for them, and re-layouts: 7.33 us -> 11.5 us
    dot_general x10 -> x0, matrix products: 24.1 us -> none  [the longest x1 4.4 us: body(): jnp.dot(enc_normed.reshape(-1, width), w_enc, preferred_element_type=F32)]
    pallas_call x5 -> x1, Pallas kernels: 211 us -> 195 us  [layer(): pl.pallas_call(functools.partial(layer_kernel, n_seq, n_nbr, tuple(scratc...]
    psum x1 -> x0, blocking collectives: 10.1 us -> none  [body(): lax.psum(jnp.dot(before, w_cond, preferred_element_type=F32), 'nbr')]
    add x2 -> x0, other arithmetic: 6.85 us -> none  [total_of(): acc = acc + received[i].astype(F32)]
    unnamed x58 -> x12, local copies, waits for them, and re-layouts: 3.38 us -> 8.89 us
    ppermute x1 -> x0, starting transfers between devices: 4.96 us -> none  [shifted(): return lax.ppermute(shard, axis, pairs)]
    convert_element_type x4 -> x0, other arithmetic: 3.64 us -> none  [the longest x1 2.26 us: body(): return (out, d_hidden.astype(BF), d_enc, d_wo, d_wk, d_wv)]
    reduce_sum x6 -> x0, other arithmetic: 3.5 us -> none  [the longest x1 1.36 us: body(): inv = jnp.sum(jnp.where(member, base + rank + 1, 0), axis=0) - 1]
  transfers between devices with their start and end apart: 1 -> 0, of which waited for: 0 -> 0; matrix products, arithmetic and copies ran while one was open for 2% -> 0% of each run, Pallas kernels for 0% -> 0%
where the time goes in v1:
time: 208 us; the launch traced here: 207 us
  Pallas kernels  195 us (94%)
  local copies, waits for them, and re-layouts  11.5 us (6%)
    pallas_call x1, Pallas kernels, layer(): pl.pallas_call(functools.partial(layer_kernel, n_seq, n_nbr, tuple(scratc...  195 us
    unnamed x12, local copies, waits for them, and re-layouts  8.89 us

profile of v1, /device:TPU:0, one launch (start us, length us, event | category | flops | bytes accessed | tf_op | source)
XLA Modules:
  0.0 207.3 jit_solution(16779184651806231117)
XLA Ops:
  0.6 1.3 broadcast_in_dim.10.refs_5_
  1.9 1.3 broadcast_in_dim.4.refs_2_
  3.2 195.2 %layer.1 = (bf16[128,1024]{1,0:T(8,128)(2,1)}, bf16[128,1024]{1,0:T(8,128)(2,1)}, bf16[6,128,896]{2,1,0:T(8,128)(2,1)}, f32[512,1024]{1,0:T(8,128)}, f32[224,512]{1,0:T(8,128)}, /*index=5*/f32[224,512]{1,0:T(8,128)}) custom-call(bf16[128,1024]{1,0:T(8,128)(2,1)} %refs_0_.1, bf16[128,1024]{1,0:T(8,128)(2,1)} %refs_1_.1, ...), custom_call_target="tpu_custom_call" | custom-call | tf_op jit(solution)/shard_map/layer/pallas_call | solution.py:636
  198.5 1.7 copy.24
  200.1 0.0 copy-start
  200.1 1.8 copy.25
  201.9 2.5 %copy.26 = bf16[6,128,896]{2,1,0:T(8,128)(2,1)} copy(bf16[6,128,896]{2,1,0:T(8,128)(2,1)} %get-tuple-element.14) | data formatting | bytes 2752512
  204.5 0.0 copy-done
  204.5 0.0 copy-start.2
  204.5 0.0 copy-start.1
  204.5 1.3 copy.27
  205.8 0.0 copy-done.2
  205.8 0.8 copy.28
  206.6 0.0 copy-done.1
  206.6 0.8 copy.29
Async XLA Ops:
  200.1 4.4 %copy-start = (f32[512,1024]{1,0:T(8,128)S(1)}, f32[512,1024]{1,0:T(8,128)}, u32[]{:S(2)}) copy-start(f32[512,1024]{1,0:T(8,128)} %get-tuple-element.15) | copy-start | bytes 6291460
  204.5 1.3 copy-start.2
  204.5 2.1 %copy-start.1 = (f32[224,512]{1,0:T(8,128)S(1)}, f32[224,512]{1,0:T(8,128)}, u32[]{:S(2)}) copy-start(f32[224,512]{1,0:T(8,128)} %get-tuple-element.17) | copy-start | bytes 1376260

commit v2 on v1

--- a/solution.py
+++ b/solution.py
@@ -49,11 +49,12 @@
 
 
 def layer_kernel(n_seq, n_nbr, names, *refs):
-    hidden, d_out, gain, emb, span, e_gain, w_cond, w_enc, w_q, w_k, w_v, w_o = refs[:12]
-    out_o, dh_o, denc_o, dwo_o, dwk_o, dwv_o = refs[12:18]
-    S = dict(zip(names, refs[18:]))
+    hidden, d_out, gain, emb, span, w_cond, w_enc, w_q, w_k, w_v, w_o = refs[:11]
+    out_o, dh_o, denc_o, dwo_o, dwk_o, dwv_o = refs[11:17]
+    S = dict(zip(names, refs[17:]))
     hid, dout, gains, wq, wo, wkv = (S[k] for k in ("hid", "dout", "gains", "wq", "wo", "wkv"))
     enc, enct, kv, big, norm, rst = (S[k] for k in ("enc", "enct", "kv", "big", "norm", "rst"))
+    prob = S["prob"]
     e1, e2, e3, po, pd = (S[k] for k in ("e1", "e2", "e3", "po", "pd"))
     ro, rd, q_s, da_s, dq_s = (S[k] for k in ("ro", "rd", "q", "da", "dq"))
     att, dcol, pw, wr, dwo, dwf = (S[k] for k in ("att", "dcol", "pw", "wr", "dwo", "dwf"))
@@ -83,14 +84,15 @@
         "v": rows_of(wkv, s, wr_k).at[:, pl.ds(local, local)],
         "q": rows_of(wq, s, wr_q), "o": cols(wo, s, piece),
     }
-    source = {"h": hidden, "d": d_out, "g": gain, "k": w_k, "v": w_v, "q": w_q, "o": w_o}
+    source = {"h": hidden, "d": d_out, "g": gain.at[:, pl.ds(0, feat)], "k": w_k, "v": w_v, "q": w_q, "o": w_o}
     loads = {
         k: pltpu.make_async_copy(source[k], own[k], lsem.at[i]) for i, k in enumerate(("h", "d", "g", "k", "v", "q", "o"))
     }
     loads["c"] = pltpu.make_async_copy(w_cond, cond_v, lsem.at[7])
     loads["e"] = pltpu.make_async_copy(emb, emb_v, lsem.at[8])
     loads["w"] = pltpu.make_async_copy(w_enc, enc_v, lsem.at[9])
-    for k in ("h", "k", "v", "q", "g", "c", "d", "e", "w", "o"):
+    loads["n"] = pltpu.make_async_copy(gain.at[:, pl.ds(feat, width)], S["egain"], lsem.at[10])
+    for k in ("h", "k", "v", "q", "g", "c", "d", "e", "w", "n", "o"):
         loads[k].start()
 
     barrier = pltpu.get_barrier_semaphore()
@@ -163,16 +165,19 @@
         part = half(a, j, h)
         return remote(part, part, ps.at[i, k, d], pr.at[i, k, d], core)
 
-    def relay(a, k):
+    def relay(a, k, kind="all"):
         i = order.index(a)
         for d in (0, 1):
-            @pl.when(valid(d, k))
+            onward = guard(d, k + 1) if k + 1 < n_seq else valid(d, k) & (s < 0)
+            when = {"all": valid(d, k), "on": onward, "end": valid(d, k) & jnp.logical_not(onward)}[kind]
+
+            @pl.when(when)
             def _(d=d):
                 part = half(a, s - k if d == 0 else s + k, b)
                 remote(part, part, zs.at[i, k, d], zr.at[i, k, d], left if d == 0 else right).wait_recv()
                 share(a, k, d, b).start()
 
-            if k + 1 < n_seq:
+            if k + 1 < n_seq and kind != "end":
                 @pl.when(guard(d, k + 1))
                 def _(d=d):
                     ring(a, k + 1, d).start()
@@ -187,7 +192,7 @@
     def wave(w, skip=()):
         for a, lag in (("k", 0), ("v", 0), ("q", 1), ("o", 2)):
             if 1 <= w - lag < n_seq and a not in skip:
-                relay(a, w - lag)
+                relay(a, w - lag, "on" if a == "o" else "all")
 
     for a in ("k", "v", "q"):
         launch(a)
@@ -238,7 +243,8 @@
 
     loads["e"].wait()
     loads["w"].wait()
-    gain_row = e_gain[...].astype(F32)
+    loads["n"].wait()
+    gain_row = S["egain"][0:1].astype(F32)
     for j in range(slots):
         mark = jnp.full((1, width), span[n * slots + j], jnp.int32)
         vals = emb_v[j].astype(F32)
@@ -342,53 +348,53 @@
         for j in range(1, total):
             at = at + (inv[j] == i).astype(jnp.int32) * j
         big[i] = kv[at]
-    wave(n_seq + 1)
-    arrived("o")
-
-    def z_sends():
-        found = []
-        for k in range(1, n_seq):
-            peer = lax.rem(s + k, n_seq)
-            found.append(remote(cols(dout, peer, piece), rows_of(dcol, s, tokens), ks.at[0, k], kr.at[0, k], {"seq": peer}))
-        return found
-
-    dcol_sends = z_sends()
-    for c in dcol_sends:
-        c.start()
-    dcol[pl.ds(pl.multiple_of(s * tokens, tokens), tokens), :] = dout[:, pl.ds(pl.multiple_of(s * piece, 128), piece)]
-
-    def d_context(c):
-        da_s[:, pl.ds(c, TILE)] = dot(dout[...], wo[pl.ds(c, TILE), :], NT).astype(BF)
-
-    tiles(local, TILE, d_context)
 
     keys = KMAX * NLEN
     factor = HD ** (-0.5)
     tok0 = pl.multiple_of(s * tokens, tokens)
 
-    def head(h, _):
+    spot = lax.broadcasted_iota(jnp.int32, (1, keys), 1)
+    bias = [jnp.where(spot < run[c] * NLEN, 0.0, -1e30) for c in range(spans)]
+
+    def forward(h, _):
         hc = pl.ds(pl.multiple_of(h * HD, HD), HD)
         vc = pl.ds(pl.multiple_of(local + h * HD, HD), HD)
         for c in range(spans):
-            tr, kr_, gr = pl.ds(c * CLEN, CLEN), pl.ds(c * KMAX, KMAX), pl.ds((spans + c) * KMAX, KMAX)
-            q, da = q_s[tr, hc], da_s[tr, hc]
-            k, v = big[kr_, :, hc].reshape(keys, HD), big[kr_, :, vc].reshape(keys, HD)
-            scores = dot(q, k, NT) * factor
-            spot = lax.broadcasted_iota(jnp.int32, scores.shape, 1)
-            scores = jnp.where(spot < run[c] * NLEN, scores, -1e30)
+            kc = pl.ds(c * KMAX, KMAX)
+            k, v = big[kc, :, hc].reshape(keys, HD), big[kc, :, vc].reshape(keys, HD)
+            scores = dot(q_s[pl.ds(c * CLEN, CLEN), hc], k, NT) * factor + bias[c]
             weights = jnp.exp(scores - jnp.max(scores, axis=-1, keepdims=True))
-            probs = weights / jnp.sum(weights, axis=-1, keepdims=True)
-            probs_b = probs.astype(BF)
-            att[pl.ds(pl.multiple_of(tok0 + c * CLEN, CLEN), CLEN), hc] = mm(probs_b, v).astype(BF)
+            probs = weights * (1.0 / jnp.sum(weights, axis=-1, keepdims=True))
+            prob[c, h] = probs
+            att[pl.ds(pl.multiple_of(tok0 + c * CLEN, CLEN), CLEN), hc] = mm(probs.astype(BF), v).astype(BF)
+        return 0
+
+    lax.fori_loop(0, heads, forward, 0)
+    for k in range(1, n_seq):
+        relay("o", k, "end")
+    arrived("o")
+
+    def d_context(c):
+        da_s[:, pl.ds(c, TILE)] = dot(dout[...], wo[pl.ds(c, TILE), :], NT).astype(BF)
+
+    tiles(local, TILE, d_context)
+
+    def backward(h, _):
+        hc = pl.ds(pl.multiple_of(h * HD, HD), HD)
+        vc = pl.ds(pl.multiple_of(local + h * HD, HD), HD)
+        for c in range(spans):
+            tr, kc, gc = pl.ds(c * CLEN, CLEN), pl.ds(c * KMAX, KMAX), pl.ds((spans + c) * KMAX, KMAX)
+            q, da, probs = q_s[tr, hc], da_s[tr, hc], prob[c, h]
+            k, v = big[kc, :, hc].reshape(keys, HD), big[kc, :, vc].reshape(keys, HD)
             d_probs = dot(da, v, NT)
             row_dot = jnp.sum(probs * d_probs, axis=-1, keepdims=True)
             d_scores = (probs * (d_probs - row_dot) * factor).astype(BF)
             dq_s[tr, hc] = mm(d_scores, k).astype(BF)
-            big[gr, :, hc] = dot(d_scores, q, TN).astype(BF).reshape(KMAX, NLEN, HD)
-            big[gr, :, vc] = dot(probs_b, da, TN).astype(BF).reshape(KMAX, NLEN, HD)
+            big[gc, :, hc] = dot(d_scores, q, TN).astype(BF).reshape(KMAX, NLEN, HD)
+            big[gc, :, vc] = dot(probs.astype(BF), da, TN).astype(BF).reshape(KMAX, NLEN, HD)
         return 0
 
-    lax.fori_loop(0, heads, head, 0)
+    lax.fori_loop(0, heads, backward, 0)
 
     att_own = rows_of(att, s, tokens)
     att_sends = [
@@ -460,6 +466,19 @@
         w_sends.append(remote(rows_of(pw, peer, wr_k), wr.at[k], ks.at[2, k], kr.at[2, k], {"seq": peer}))
     for c in w_sends:
         c.start()
+
+    def z_sends():
+        found = []
+        for k in range(1, n_seq):
+            peer = lax.rem(s + k, n_seq)
+            found.append(remote(cols(dout, peer, piece), rows_of(dcol, s, tokens), ks.at[0, k], kr.at[0, k], {"seq": peer}))
+        return found
+
+    dcol_sends = z_sends()
+    for c in dcol_sends:
+        c.start()
+    dcol[pl.ds(pl.multiple_of(s * tokens, tokens), tokens), :] = dout[:, pl.ds(pl.multiple_of(s * piece, 128), piece)]
+
 
     for h in (0, 1):
         back((n ^ 1, n ^ 2)[h], h * half_slots)
@@ -592,9 +611,9 @@
         c.wait()
 
 
-def layer(hidden, d_out, gain, emb, span, e_gain, w_cond, w_enc, w_q, w_k, w_v, w_o):
+def layer(hidden, d_out, gain, emb, span, w_cond, w_enc, w_q, w_k, w_v, w_o):
     n_seq, n_nbr = lax.axis_size("seq"), lax.axis_size("nbr")
-    args = (hidden, d_out, gain, emb, span, e_gain, w_cond, w_enc, w_q, w_k, w_v, w_o)
+    args = (hidden, d_out, gain, emb, span, w_cond, w_enc, w_q, w_k, w_v, w_o)
     tokens, feat = hidden.shape
     slots, _, width = emb.shape
     total = slots * n_nbr
@@ -604,11 +623,11 @@
     vm = pltpu.VMEM
     dma = pltpu.SemaphoreType.DMA
     scratch = dict(
-        hid=vm((tokens, full), BF), dout=vm((tokens, full), BF), gains=vm((n_nbr,) + gain.shape, BF),
+        hid=vm((tokens, full), BF), dout=vm((tokens, full), BF), gains=vm((n_nbr, gain.shape[0], feat), BF), egain=vm((gain.shape[0], width), BF),
         wq=vm((full, local), BF), wo=vm((local, full), BF), wkv=vm((width, 2 * local), BF),
         enc=vm((total * NLEN, width), BF), enct=vm((width, total * NLEN), BF),
         kv=vm((total, NLEN, 2 * local), BF), big=vm((2 * spans * KMAX, NLEN, 2 * local), BF),
-        norm=vm((tokens, full), BF), rst=vm((tokens, HD), F32),
+        norm=vm((tokens, full), BF), prob=vm((spans, local // HD, CLEN, KMAX * NLEN), F32), rst=vm((tokens, HD), F32),
         e1=vm(emb.shape, BF), e2=vm(emb.shape, BF), e3=vm(emb.shape, BF),
         po=vm((n_nbr, tokens, feat), BF), pd=vm((n_nbr, tokens, feat), BF),
         ro=vm((3, 2, tokens // 2, feat), BF), rd=vm((3, 2, tokens // 2, feat), BF),
@@ -619,15 +638,14 @@
         emb=vm(emb.shape, BF), cond=vm(w_cond.shape, BF), wenc=vm(w_enc.shape, BF),
         pool=vm((2, 8, feat), F32), cpart=vm((8, width), F32), crecv=vm((3, 8, width), F32),
         st=vm((5, tokens, HD), F32),
-        lsem=dma((10,)), osem=dma((slots + 8,)),
+        lsem=dma((11,)), osem=dma((slots + 8,)),
         zs=dma((4, n_seq, 2)), zr=dma((4, n_seq, 2)), ps=dma((4, n_seq, 2)), pr=dma((4, n_seq, 2)),
         ns=dma((3, 4)), nr=dma((3, 4)), es=dma((slots, 3)), er=dma((slots, 3)),
         ss=dma((7,)), sr=dma((7,)), us=dma((slots + 4, 3)), ur=dma((slots + 4, 3)),
         ks=dma((3, n_seq)), kr=dma((3, n_seq)),
     )
-    specs = [ANY] * 12
+    specs = [ANY] * 11
     specs[4] = pl.BlockSpec(memory_space=pltpu.SMEM)
-    specs[5] = pl.BlockSpec(memory_space=pltpu.VMEM)
     shapes = [
         jax.ShapeDtypeStruct(hidden.shape, BF), jax.ShapeDtypeStruct(hidden.shape, BF),
         jax.ShapeDtypeStruct(emb.shape, BF), jax.ShapeDtypeStruct(w_o.shape, F32),
@@ -646,11 +664,40 @@
     )(*args)
 
 
+def settle_kernel(*refs):
+    count = len(refs) // 3
+    ins, outs, bufs = refs[:count], refs[count : 2 * count], refs[2 * count : 3 * count]
+    sems = refs[3 * count]
+    loads = [pltpu.make_async_copy(a, v, sems.at[0, i]) for i, (a, v) in enumerate(zip(ins, bufs))]
+    stores = [pltpu.make_async_copy(v, o, sems.at[1, i]) for i, (v, o) in enumerate(zip(bufs, outs))]
+    for c in loads:
+        c.start()
+    for a, c in zip(loads, stores):
+        a.wait()
+        c.start()
+    for c in stores:
+        c.wait()
+
+
+def settle(*arrays):
+    count = len(arrays)
+    return pl.pallas_call(
+        settle_kernel,
+        out_shape=[jax.ShapeDtypeStruct(v.shape, v.dtype) for v in arrays],
+        in_specs=[ANY] * count,
+        out_specs=[ANY] * count,
+        scratch_shapes=[pltpu.VMEM(v.shape, v.dtype) for v in arrays] + [pltpu.SemaphoreType.DMA((2, count))],
+        compiler_params=pltpu.CompilerParams(vmem_limit_bytes=60 * 2**20),
+        name="settle",
+    )(*arrays)
+
+
 def body(hidden, d_out, nbr_emb, slot_span, dec_gain, enc_gain, w_cond, w_enc, w_q, w_k, w_v, w_o):
-    gain = jnp.broadcast_to(dec_gain[None], (16, dec_gain.shape[0]))
-    return tuple(layer(
-        hidden, d_out, gain, nbr_emb, slot_span, enc_gain[None], w_cond, w_enc, w_q, w_k, w_v, w_o
-    ))
+    both = jnp.concatenate([dec_gain, enc_gain])
+    gain = jnp.broadcast_to(both[None], (16, both.shape[0]))
+    return tuple(settle(*layer(
+        hidden, d_out, gain, nbr_emb, slot_span, w_cond, w_enc, w_q, w_k, w_v, w_o
+    )))
 
 
 def solution(mesh):

time: 208 us -> 180 us (0.87)
  Pallas kernels: 195 us -> 177 us
  local copies, waits for them, and re-layouts: 11.5 us -> 0.63 us
    pallas_call x1, Pallas kernels: 195 us -> 173 us  [layer(): pl.pallas_call(functools.partial(layer_kernel, n_seq, n_nbr, tuple(scratc...]
    unnamed x12 -> x0, local copies, waits for them, and re-layouts: 8.89 us -> none
    pallas_call x0 -> x1, Pallas kernels: none -> 4.09 us  [settle(): pl.pallas_call(settle_kernel, out_shape=[jax.ShapeDtypeStruct(v.shape, v....]
where the time goes in v2:
time: 180 us; the launch traced here: 179 us
  Pallas kernels  177 us (98%)
    pallas_call x1, Pallas kernels, layer(): pl.pallas_call(functools.partial(layer_kernel, n_seq, n_nbr, tuple(scratc...  173 us
    pallas_call x1, Pallas kernels, settle(): pl.pallas_call(settle_kernel, out_shape=[jax.ShapeDtypeStruct(v.shape, v....  4.09 us

profile of v2, /device:TPU:0, one launch (start us, length us, event | category | flops | bytes accessed | tf_op | source)
XLA Modules:
  0.0 179.2 jit_solution(3576330393929214932)
XLA Ops:
  0.6 0.7 pad_maximum_fusion
  1.3 0.6 broadcast_in_dim.2.refs_2_
  2.0 172.9 %layer.1 = (bf16[128,1024]{1,0:T(8,128)(2,1)}, bf16[128,1024]{1,0:T(8,128)(2,1)}, bf16[6,128,896]{2,1,0:T(8,128)(2,1)}, f32[512,1024]{1,0:T(8,128)}, f32[224,512]{1,0:T(8,128)}, /*index=5*/f32[224,512]{1,0:T(8,128)}) custom-call(bf16[128,1024]{1,0:T(8,128)(2,1)} %refs_0_.1, bf16[128,1024]{1,0:T(8,128)(2,1)} %refs_1_.1, ...), custom_call_target="tpu_custom_call" | custom-call | tf_op jit(solution)/shard_map/layer/pallas_call | solution.py:654
  174.9 4.1 %settle.1 = (bf16[128,1024]{1,0:T(8,128)(2,1)}, bf16[128,1024]{1,0:T(8,128)(2,1)}, bf16[6,128,896]{2,1,0:T(8,128)(2,1)}, f32[512,1024]{1,0:T(8,128)}, f32[224,512]{1,0:T(8,128)}, /*index=5*/f32[224,512]{1,0:T(8,128)}) custom-call(bf16[128,1024]{1,0:T(8,128)(2,1)} %get-tuple-element.12.refs_0_, bf16[128,1024]{1,0:T(8,128)(2,1)} %get-tuple-element.13.refs_1_, ...), custom_call_target="tpu_custom_call" | custom-call | tf_op jit(solution)/shard_map/settle/pallas_call | solution.py:684

commit v3 on v2

--- a/solution.py
+++ b/solution.py
@@ -54,8 +54,8 @@
     S = dict(zip(names, refs[17:]))
     hid, dout, gains, wq, wo, wkv = (S[k] for k in ("hid", "dout", "gains", "wq", "wo", "wkv"))
     enc, enct, kv, big, norm, rst = (S[k] for k in ("enc", "enct", "kv", "big", "norm", "rst"))
-    prob = S["prob"]
-    e1, e2, e3, po, pd = (S[k] for k in ("e1", "e2", "e3", "po", "pd"))
+    prob, dsend, drecv = S["prob"], S["dsend"], S["drecv"]
+    e1, e2, e3, po, pd = (S[k] for k in ("emb", "e2", "e3", "po", "pd"))
     ro, rd, q_s, da_s, dq_s = (S[k] for k in ("ro", "rd", "q", "da", "dq"))
     att, dcol, pw, wr, dwo, dwf = (S[k] for k in ("att", "dcol", "pw", "wr", "dwo", "dwf"))
     emb_v, cond_v, enc_v, pool = (S[k] for k in ("emb", "cond", "wenc", "pool"))
@@ -152,8 +152,9 @@
     def valid(d, k):
         return (s - k >= 0) if d == 0 else (s + k < n_seq)
 
-    def launch(a):
-        loads[a].wait()
+    def launch(a, ready=False):
+        if not ready:
+            loads[a].wait()
         for d in (0, 1):
             @pl.when(guard(d, 1))
             def _(a=a, d=d):
@@ -190,9 +191,9 @@
                     share(a, k, d, 1 - b).wait_recv()
 
     def wave(w, skip=()):
-        for a, lag in (("k", 0), ("v", 0), ("q", 1), ("o", 2)):
+        for a, lag in (("k", 0), ("v", 0), ("q", 1)):
             if 1 <= w - lag < n_seq and a not in skip:
-                relay(a, w - lag, "on" if a == "o" else "all")
+                relay(a, w - lag)
 
     for a in ("k", "v", "q"):
         launch(a)
@@ -241,6 +242,15 @@
         part = enc.at[slot_rows(src, j)]
         return remote(part, part, es.at[j, i], er.at[j, i], dev)
 
+    def diagonal(ref, i):
+        c = tokens // 2
+        for d, (src, dev) in enumerate(((n ^ 1, y), (n ^ 2, x))):
+            full = cols(ref, src, feat)
+            remote(full, full, ns.at[i, d], nr.at[i, d], dev).wait_recv()
+            part = full.at[pl.ds(d * c, c)]
+            remote(part, part, ns.at[i, 2 + d], nr.at[i, 2 + d], dev).start()
+
+    diagonal(hid, 0)
     loads["e"].wait()
     loads["w"].wait()
     loads["n"].wait()
@@ -255,17 +265,10 @@
         enc[slot_rows(n, j), :] = (vals + mixed / (1.0 + jnp.exp(-mixed))).astype(BF)
         slot_copy(n, j, 0, x).start()
         slot_copy(n, j, 1, y).start()
+        if j == 1:
+            diagonal(dout, 1)
         if j == half_slots:
             wave(1)
-            launch("o")
-
-    def diagonal(ref, i):
-        c = tokens // 2
-        for d, (src, dev) in enumerate(((n ^ 1, y), (n ^ 2, x))):
-            full = cols(ref, src, feat)
-            remote(full, full, ns.at[i, d], nr.at[i, d], dev).wait_recv()
-            part = full.at[pl.ds(d * c, c)]
-            remote(part, part, ns.at[i, 2 + d], nr.at[i, 2 + d], dev).start()
 
     def diagonal_done(ref, i):
         c = tokens // 2
@@ -291,13 +294,34 @@
 
         tiles(2 * local, TILE, tile)
 
-    diagonal(hid, 0)
-    diagonal(dout, 1)
     wave(2)
+    diagonal_done(dout, 1)
+    def z_sends():
+        found = []
+        for k in range(1, n_seq):
+            peer = lax.rem(s + k, n_seq)
+            found.append(remote(cols(dout, peer, piece), rows_of(dcol, s, tokens), ks.at[4, k], kr.at[4, k], {"seq": peer}))
+        return found
+
+    dcol_sends = z_sends()
+    def edge(i):
+        return (i == 0) | (i == n_seq - 1)
+
+    def columns(late):
+        for k in range(1, n_seq):
+            delayed = edge(lax.rem(s + k, n_seq)) & jnp.logical_not(edge(s))
+
+            @pl.when(delayed if late else jnp.logical_not(delayed))
+            def _(k=k):
+                dcol_sends[k - 1].start()
+
+    columns(False)
+    dcol[pl.ds(pl.multiple_of(s * tokens, tokens), tokens), :] = dout[:, pl.ds(pl.multiple_of(s * piece, 128), piece)]
+
+
     for j in range(half_slots):
         pass_on(j)
     diagonal_done(hid, 0)
-    diagonal_done(dout, 1)
     for c in gain_sends:
         c.wait_recv()
 
@@ -319,6 +343,29 @@
     arrived("v")
     for m in (n, n ^ 1, n ^ 2):
         project(m, 0)
+
+    columns(True)
+    loads["o"].wait()
+
+    def da_copy(k):
+        peer = lax.rem(s + n_seq - k, n_seq)
+        return remote(dsend.at[k], drecv.at[k], ks.at[3, k], kr.at[3, k], {"seq": peer})
+
+    def da_parts(late):
+        for i in range(1, n_seq):
+            k = i + (n_seq - 2 * i) * (s > 0).astype(jnp.int32)
+            peer = lax.rem(s + n_seq - k, n_seq)
+            delayed = edge(s) & jnp.logical_not(edge(peer))
+
+            @pl.when(delayed if late else jnp.logical_not(delayed))
+            def _(k=k, peer=peer):
+                rows = rows_of(dcol, peer, tokens)
+                remote(rows, rows, ks.at[4, k], kr.at[4, k], {"seq": peer}).wait_recv()
+                part = dot(rows[...], wo[:, pl.ds(pl.multiple_of(s * piece, 128), piece)], NT)
+                dsend[k] = part.astype(BF)
+                da_copy(k).start()
+
+    da_parts(False)
     wave(n_seq)
     for m in (n, n ^ 1, n ^ 2):
         project(m, half_slots)
@@ -370,14 +417,14 @@
         return 0
 
     lax.fori_loop(0, heads, forward, 0)
+    da_parts(True)
+    own_rows = dcol[pl.ds(tok0, tokens), :]
+    acc = dot(own_rows, wo[:, pl.ds(pl.multiple_of(s * piece, 128), piece)], NT)
     for k in range(1, n_seq):
-        relay("o", k, "end")
-    arrived("o")
-
-    def d_context(c):
-        da_s[:, pl.ds(c, TILE)] = dot(dout[...], wo[pl.ds(c, TILE), :], NT).astype(BF)
-
-    tiles(local, TILE, d_context)
+        da_copy(k).wait_recv()
+        acc = acc + drecv[k].astype(F32)
+    da_s[...] = acc.astype(BF)
+    launch("o", True)
 
     def backward(h, _):
         hc = pl.ds(pl.multiple_of(h * HD, HD), HD)
@@ -460,30 +507,28 @@
         pw[:, pl.ds(c, TILE)] = mm(enct[...], kv[:, :, pl.ds(c, TILE)].reshape(total * NLEN, TILE)).astype(BF)
 
     tiles(2 * local, TILE, d_weights)
-    w_sends = []
-    for k in range(1, n_seq):
-        peer = lax.rem(s + k, n_seq)
-        w_sends.append(remote(rows_of(pw, peer, wr_k), wr.at[k], ks.at[2, k], kr.at[2, k], {"seq": peer}))
-    for c in w_sends:
-        c.start()
-
-    def z_sends():
-        found = []
-        for k in range(1, n_seq):
-            peer = lax.rem(s + k, n_seq)
-            found.append(remote(cols(dout, peer, piece), rows_of(dcol, s, tokens), ks.at[0, k], kr.at[0, k], {"seq": peer}))
-        return found
-
-    dcol_sends = z_sends()
-    for c in dcol_sends:
-        c.start()
-    dcol[pl.ds(pl.multiple_of(s * tokens, tokens), tokens), :] = dout[:, pl.ds(pl.multiple_of(s * piece, 128), piece)]
-
+
+    def w_copy(d, i):
+        place = i if d == 0 else i + (n_seq - i) * (s - 1 == i).astype(jnp.int32)
+        dev = right if d == 0 else left
+        return remote(rows_of(pw, i, wr_k), wr.at[place], ks.at[d * 2, i], kr.at[d * 2, i], dev)
+
+    def w_sends_on(d, i):
+        return (s < i) if d == 0 else (s > i)
+
+    w_steps = []
+    for i in range(n_seq - 1):
+        w_steps += [(0, n_seq - 1 - i), (1, i)]
+    for d, i in w_steps:
+        @pl.when(w_sends_on(d, i) & ((s == 0) if d == 0 else (s == n_seq - 1)))
+        def _(d=d, i=i):
+            w_copy(d, i).start()
 
     for h in (0, 1):
         back((n ^ 1, n ^ 2)[h], h * half_slots)
         for j in sets[h]:
             enc_sums[j].copy(1).start()
+    relay("o", 1, "on")
 
     def out_part(m):
         def tile(c):
@@ -499,7 +544,7 @@
 
         tiles(feat, TILE, tile)
 
-    for make, group in ((out_part, out_sums), (dn_part, dn_sums)):
+    def sum_parts(make, group):
         make(n ^ 3)
         for u in group:
             u.copy(0).start()
@@ -509,6 +554,8 @@
             u.copy(1).start()
         make(n)
 
+    sum_parts(dn_part, dn_sums)
+
     def stat_rows(r):
         acc = jnp.zeros((32, 1), F32)
         for m in range(n_nbr):
@@ -526,15 +573,29 @@
     ]
     for c in stat_sends:
         c.start()
+    for k in range(2, n_seq):
+        relay("o", k, "on")
 
     for h in (0, 1):
         back((n ^ 2, n ^ 1)[h], h * half_slots)
     for i in range(half_slots):
         enc_sums[i].second()
         enc_sums[half_slots + i].second()
+    for d, i in w_steps:
+        @pl.when(w_sends_on(d, i) & ((s > 0) if d == 0 else (s < n_seq - 1)))
+        def _(d=d, i=i):
+            w_copy(d, i).wait_recv()
+            mine = rows_of(pw, i, wr_k)
+            mine[...] = (mine[...].astype(F32) + wr[i].astype(F32)).astype(BF)
+            w_copy(d, i).start()
+
+    for k in range(1, n_seq):
+        relay("o", k, "end")
+    arrived("o")
+    sum_parts(out_part, out_sums)
     for h in (0, 1):
         back(n, h * half_slots)
-    for u in out_sums + dn_sums:
+    for u in dn_sums + out_sums:
         u.second()
 
     writes = []
@@ -544,7 +605,7 @@
         c.start()
         writes.append(c)
 
-    for c in dcol_sends + att_sends:
+    for c in att_sends:
         c.wait_recv()
 
     step = min(TILE, piece)
@@ -555,12 +616,18 @@
     tiles(piece, step, d_out_weights)
     write(dwo, dwo_o)
 
-    for c in w_sends:
-        c.wait_recv()
-    acc = rows_of(pw, s, wr_k)[...].astype(F32)
-    for k in range(1, n_seq):
-        acc = acc + wr[k].astype(F32)
-    dwf[...] = acc
+    dwf[...] = rows_of(pw, s, wr_k)[...].astype(F32)
+
+    @pl.when(has_left)
+    def _():
+        remote(wr.at[s], wr.at[s], ks.at[0, s], kr.at[0, s], left).wait_recv()
+        dwf[...] = dwf[...] + wr[s].astype(F32)
+
+    @pl.when(has_right)
+    def _():
+        remote(wr.at[n_seq], wr.at[n_seq], ks.at[2, s], kr.at[2, s], right).wait_recv()
+        dwf[...] = dwf[...] + wr[n_seq].astype(F32)
+
     write(dwf.at[:, pl.ds(0, local)], dwk_o)
     write(dwf.at[:, pl.ds(local, local)], dwv_o)
 
@@ -599,8 +666,13 @@
                 @pl.when(guard(d, k))
                 def _(a=a, k=k, d=d):
                     ring(a, k, d).wait_send()
-    for c in pair("h", 0) + pair("d", 1) + gain_sends + sums + stat_sends + dcol_sends + att_sends + w_sends:
+    for c in pair("h", 0) + pair("d", 1) + gain_sends + sums + stat_sends + dcol_sends + [da_copy(k) for k in range(1, n_seq)] + att_sends:
         c.wait_send()
+    for d, i in w_steps:
+        @pl.when(w_sends_on(d, i))
+        def _(d=d, i=i):
+            w_copy(d, i).wait_send()
+
     for j in range(slots):
         for i in range(3):
             slot_copy(n, j, i, x).wait_send()
@@ -628,12 +700,12 @@
         enc=vm((total * NLEN, width), BF), enct=vm((width, total * NLEN), BF),
         kv=vm((total, NLEN, 2 * local), BF), big=vm((2 * spans * KMAX, NLEN, 2 * local), BF),
         norm=vm((tokens, full), BF), prob=vm((spans, local // HD, CLEN, KMAX * NLEN), F32), rst=vm((tokens, HD), F32),
-        e1=vm(emb.shape, BF), e2=vm(emb.shape, BF), e3=vm(emb.shape, BF),
+        e2=vm(emb.shape, BF), e3=vm(emb.shape, BF),
         po=vm((n_nbr, tokens, feat), BF), pd=vm((n_nbr, tokens, feat), BF),
         ro=vm((3, 2, tokens // 2, feat), BF), rd=vm((3, 2, tokens // 2, feat), BF),
         q=vm((tokens, local), BF), da=vm((tokens, local), BF), dq=vm((tokens, local), BF),
         att=vm((n_seq * tokens, local), BF), dcol=vm((n_seq * tokens, piece), BF),
-        pw=vm((width, 2 * local), BF), wr=vm((n_seq, wr_k, 2 * local), BF),
+        pw=vm((width, 2 * local), BF), wr=vm((n_seq + 1, wr_k, 2 * local), BF),
         dwo=vm((local, piece), F32), dwf=vm((wr_k, 2 * local), F32),
         emb=vm(emb.shape, BF), cond=vm(w_cond.shape, BF), wenc=vm(w_enc.shape, BF),
         pool=vm((2, 8, feat), F32), cpart=vm((8, width), F32), crecv=vm((3, 8, width), F32),
@@ -642,7 +714,8 @@
         zs=dma((4, n_seq, 2)), zr=dma((4, n_seq, 2)), ps=dma((4, n_seq, 2)), pr=dma((4, n_seq, 2)),
         ns=dma((3, 4)), nr=dma((3, 4)), es=dma((slots, 3)), er=dma((slots, 3)),
         ss=dma((7,)), sr=dma((7,)), us=dma((slots + 4, 3)), ur=dma((slots + 4, 3)),
-        ks=dma((3, n_seq)), kr=dma((3, n_seq)),
+        ks=dma((5, n_seq)), kr=dma((5, n_seq)),
+        dsend=vm((n_seq, tokens, local), BF), drecv=vm((n_seq, tokens, local), BF),
     )
     specs = [ANY] * 11
     specs[4] = pl.BlockSpec(memory_space=pltpu.SMEM)

time: 180 us -> 170 us (0.944)
  Pallas kernels: 177 us -> 165 us
    pallas_call x1, Pallas kernels: 173 us -> 161 us  [layer(): pl.pallas_call(functools.partial(layer_kernel, n_seq, n_nbr, tuple(scratc...]
where the time goes in v3:
time: 170 us; the launch traced here: 167 us
  Pallas kernels  165 us (97%)
    pallas_call x1, Pallas kernels, layer(): pl.pallas_call(functools.partial(layer_kernel, n_seq, n_nbr, tuple(scratc...  161 us
    pallas_call x1, Pallas kernels, settle(): pl.pallas_call(settle_kernel, out_shape=[jax.ShapeDtypeStruct(v.shape, v....  4.09 us

profile of v3, /device:TPU:0, one launch (start us, length us, event | category | flops | bytes accessed | tf_op | source)
XLA Modules:
  0.0 167.5 jit_solution(8611998296335005595)
XLA Ops:
  0.6 0.7 pad_maximum_fusion
  1.3 0.6 broadcast_in_dim.2.refs_2_
  2.0 161.2 %layer.1 = (bf16[128,1024]{1,0:T(8,128)(2,1)}, bf16[128,1024]{1,0:T(8,128)(2,1)}, bf16[6,128,896]{2,1,0:T(8,128)(2,1)}, f32[512,1024]{1,0:T(8,128)}, f32[224,512]{1,0:T(8,128)}, /*index=5*/f32[224,512]{1,0:T(8,128)}) custom-call(bf16[128,1024]{1,0:T(8,128)(2,1)} %refs_0_.1, bf16[128,1024]{1,0:T(8,128)(2,1)} %refs_1_.1, ...), custom_call_target="tpu_custom_call" | custom-call | tf_op jit(solution)/shard_map/layer/pallas_call | solution.py:727
  163.2 4.1 %settle.1 = (bf16[128,1024]{1,0:T(8,128)(2,1)}, bf16[128,1024]{1,0:T(8,128)(2,1)}, bf16[6,128,896]{2,1,0:T(8,128)(2,1)}, f32[512,1024]{1,0:T(8,128)}, f32[224,512]{1,0:T(8,128)}, /*index=5*/f32[224,512]{1,0:T(8,128)}) custom-call(bf16[128,1024]{1,0:T(8,128)(2,1)} %get-tuple-element.12.refs_0_, bf16[128,1024]{1,0:T(8,128)(2,1)} %get-tuple-element.13.refs_1_, ...), custom_call_target="tpu_custom_call" | custom-call | tf_op jit(solution)/shard_map/settle/pallas_call | solution.py:757
